TPU v7x, 32 devices: a whole 2x2x4 slice. The times are simulated.
32 devices in a mesh: dp: 8 (over z, x), seq: 4 (over y, core).
Axes of the slice: x: 2, y: 2, z: 4, core: 2. Of those that a mesh axis runs over, the one named last changes fastest.
Arguments:
- tokens: bfloat16 [4608, 3584], P('dp'), may hold values from -6 to 6
- positions: int32 [3, 4608], P(None, 'dp'), may hold values from 0 to 2047
- loss_mask: int32 [4608], P('dp'), may hold values from 0 to 1, as said below
- sample_tokens: int32 [8, 3], replicated, may hold values from 96 to 384, as said below
- dest_slot: int32 [4608], P('dp'), may hold values from 0 to 6143, as said below
- norm_gain: float32 [3584], replicated, may hold values from 0.5 to 1.5
- q_weight: bfloat16 [3584, 2048], P(None, 'seq'), may hold values from -0.09375 to 0.09375
- k_weight: bfloat16 [3584, 512], P(None, 'seq'), may hold values from -0.09375 to 0.09375
- v_weight: bfloat16 [3584, 512], P(None, 'seq'), may hold values from -0.09375 to 0.09375
- q_bias: float32 [2048], P('seq'), may hold values from -3 to 3
- k_bias: float32 [512], P('seq'), may hold values from -3 to 3
- v_bias: float32 [512], P('seq'), may hold values from -3 to 3
- o_weight: bfloat16 [2048, 3584], P('seq'), may hold values from -0.125 to 0.125
Outputs:
- mixed: bfloat16 [6144, 3584], P(('dp', 'seq'))
- token_weight: float32 [6144], P(('dp', 'seq'))
Inputs may be any that keep to these rules, and one draw needn't show every extreme that they name: `sample_tokens`: row r gives the token counts of the samples in the buckets of receiver r, of 384, 192 and 192 slots; each count lies between half of its bucket's slots and all of them. Some receiver has all three buckets full. All counts together equal the number of rows of tokens. `dest_slot`: every row has a slot of its own, and the slots that rows take are exactly the first sample_tokens[r, b] slots of each bucket b of each receiver r. Of the rows of one sender at most 96 go to one receiver; a receiver whose buckets are all full takes exactly 96 rows from every sender. `loss_mask`: the first of each sender's 576 rows is 1.
All inputs are finite; a program needn't handle non-finite values.
Results may differ from a plain program's by a relative error of at most 0.015.
Values may be sent and summed in bfloat16 or wider, within the bound.
No kernel may reach another device: no remote copies, remote signals or barrier semaphores. Data moves between devices by JAX's collectives and lax.ppermute only.
A program may use at most 128 MiB of HBM per device.

v0:
```python
import math

import jax
import jax.numpy as jnp
from jax import lax
from jax.sharding import PartitionSpec as P

DH = 128
BUCKET = 384


NORM_EPSILON = 1e-06
ROPE_BASE = 1000000.0


def rms_norm(rows_in, gain):
    widened = rows_in.astype(jnp.float32)
    mean_square = jnp.mean(widened * widened, axis=-1, keepdims=True)
    return (widened * lax.rsqrt(mean_square + NORM_EPSILON) * gain).astype(jnp.bfloat16)


def rotary_tables(position_ids, head_size):
    half_size = head_size // 2
    pair_index = jnp.arange(half_size, dtype=jnp.int32)
    inv_freq = jnp.exp(pair_index.astype(jnp.float32) * (-2.0 * math.log(ROPE_BASE) / head_size))
    time_limit = head_size // 8
    height_limit = time_limit + 3 * head_size // 16
    chosen = jnp.where(
        pair_index[None, :] < time_limit,
        position_ids[0][:, None],
        jnp.where(
            pair_index[None, :] < height_limit, position_ids[1][:, None], position_ids[2][:, None]
        ),
    )
    angles = chosen.astype(jnp.float32) * inv_freq[None, :]
    return (jnp.cos(angles), jnp.sin(angles))


def rotate(heads_in, cosine, sine_part):
    half_size = heads_in.shape[-1] // 2
    first_half = heads_in[..., :half_size]
    second_half = heads_in[..., half_size:]
    cosine = cosine[:, None, :]
    sine_part = sine_part[:, None, :]
    return jnp.concatenate(
        [
            first_half * cosine - second_half * sine_part,
            second_half * cosine + first_half * sine_part,
        ],
        axis=-1,
    )


def project(normed, q_weight, k_weight, v_weight, q_bias, k_bias, v_bias):
    queries = (jnp.dot(normed, q_weight, preferred_element_type=jnp.float32) + q_bias).astype(
        jnp.bfloat16
    )
    key_rows = (jnp.dot(normed, k_weight, preferred_element_type=jnp.float32) + k_bias).astype(
        jnp.bfloat16
    )
    value_rows = (jnp.dot(normed, v_weight, preferred_element_type=jnp.float32) + v_bias).astype(
        jnp.bfloat16
    )
    return (queries, key_rows, value_rows)


def rotate_rows(queries, key_rows, position_ids):
    cosine, sine_part = rotary_tables(position_ids, DH)
    row_count = queries.shape[0]
    q_turned = rotate(queries.astype(jnp.float32).reshape(row_count, -1, DH), cosine, sine_part)
    k_turned = rotate(key_rows.astype(jnp.float32).reshape(row_count, -1, DH), cosine, sine_part)
    return (
        q_turned.astype(jnp.bfloat16).reshape(row_count, -1),
        k_turned.astype(jnp.bfloat16).reshape(row_count, -1),
    )


def place_rows(rows_in, target_slots, slot_count):
    flat_rows = rows_in.reshape(slot_count, -1)
    empty = jnp.zeros((slot_count, flat_rows.shape[-1]), flat_rows.dtype)
    return empty.at[target_slots].set(flat_rows, mode="drop")


def attend_group(queries, key_rows, value_rows, lengths):
    block_count = queries.shape[0]
    row_count = queries.shape[1]
    scores = jnp.einsum(
        "bqagd,bkad->bagqk", queries, key_rows, preferred_element_type=jnp.float32
    ) * (1.0 / math.sqrt(DH))
    places = jnp.arange(row_count, dtype=jnp.int32)
    allowed = (places[:, None] >= places[None, :])[None] & (
        places[None, None, :] < lengths[:, None, None]
    )
    scores = jnp.where(allowed[:, None, None], scores, -1e30)
    weights = jax.nn.softmax(scores, axis=-1).astype(jnp.bfloat16)
    context = jnp.einsum(
        "bagqk,bkad->bqagd", weights, value_rows, preferred_element_type=jnp.float32
    )
    live_rows = places[None, :] < lengths[:, None]
    context = jnp.where(live_rows[:, :, None, None, None], context, 0.0).astype(jnp.bfloat16)
    return context.reshape(block_count * row_count, -1)


def attend_buckets(q_rows, k_rows, v_rows, lengths, kv_count, group_size):
    half_bucket = BUCKET // 2
    first_part = attend_group(
        q_rows[:BUCKET].reshape(1, BUCKET, kv_count, group_size, DH),
        k_rows[:BUCKET].reshape(1, BUCKET, kv_count, DH),
        v_rows[:BUCKET].reshape(1, BUCKET, kv_count, DH),
        lengths[:1],
    )
    second_part = attend_group(
        q_rows[BUCKET:].reshape(2, half_bucket, kv_count, group_size, DH),
        k_rows[BUCKET:].reshape(2, half_bucket, kv_count, DH),
        v_rows[BUCKET:].reshape(2, half_bucket, kv_count, DH),
        lengths[1:],
    )
    return jnp.concatenate([first_part, second_part], axis=0)


def per_device(
    tokens,
    positions,
    loss_mask,
    sample_tokens,
    dest_slot,
    norm_gain,
    q_weight,
    k_weight,
    v_weight,
    q_bias,
    k_bias,
    v_bias,
    o_weight,
):
    peer_count = lax.axis_size("dp")
    own_index = lax.axis_index("dp")
    seq_count = lax.axis_size("seq")
    seq_index = lax.axis_index("seq")
    source_rows = tokens.shape[0]
    slot_count = 2 * BUCKET
    capacity = slot_count // peer_count
    head_count = q_weight.shape[1] // DH
    kv_count = k_weight.shape[1] // DH
    group_size = head_count // kv_count
    target_peer = dest_slot // slot_count
    target_local = dest_slot % slot_count
    peer_ids = jnp.arange(peer_count, dtype=jnp.int32)
    one_hot = (target_peer[:, None] == peer_ids[None, :]).astype(jnp.int32)
    ranking = jnp.sum((jnp.cumsum(one_hot, axis=0) - one_hot) * one_hot, axis=1)
    buffer_slot = target_peer * capacity + ranking
    row_ids = jnp.arange(source_rows, dtype=jnp.int32)
    source_of = jnp.zeros((slot_count,), jnp.int32).at[buffer_slot].set(row_ids)
    is_live = jnp.zeros((slot_count,), jnp.int32).at[buffer_slot].set(1) > 0
    info_rows = jnp.concatenate([positions, loss_mask[None, :], target_local[None, :]], axis=0)
    filler = jnp.array([0, 0, 0, 0, slot_count], jnp.int32)[:, None]
    send_info = jnp.where(is_live[None, :], info_rows[:, source_of], filler)
    mask_sum = jnp.sum(loss_mask)
    recv_info = lax.all_to_all(send_info, "dp", split_axis=1, concat_axis=1, tiled=True)
    loss_total = lax.psum(mask_sum.astype(jnp.float32), "dp")
    recv_local = recv_info[4]
    slot_info = (
        jnp.zeros((4, slot_count), jnp.int32).at[:, recv_local].set(recv_info[:4], mode="drop")
    )
    zero_value = jnp.zeros((), jnp.bfloat16)
    q_all, k_all, v_all = project(
        rms_norm(tokens, norm_gain), q_weight, k_weight, v_weight, q_bias, k_bias, v_bias
    )
    q_all, k_all = rotate_rows(q_all, k_all, positions)

    def select_slots(source_array):
        return jnp.where(is_live[:, None], source_array[source_of], zero_value).reshape(
            peer_count, capacity, -1
        )

    q_recv, k_recv, v_recv = (
        lax.all_to_all(select_slots(q_all), "dp", split_axis=0, concat_axis=0, tiled=True),
        lax.all_to_all(select_slots(k_all), "dp", split_axis=0, concat_axis=0, tiled=True),
        lax.all_to_all(select_slots(v_all), "dp", split_axis=0, concat_axis=0, tiled=True),
    )
    q_slots = place_rows(q_recv, recv_local, slot_count)
    k_slots = place_rows(k_recv, recv_local, slot_count)
    v_slots = place_rows(v_recv, recv_local, slot_count)
    lengths = sample_tokens[own_index]
    context = attend_buckets(q_slots, k_slots, v_slots, lengths, kv_count, group_size)
    part_rows = slot_count // seq_count
    mixed = lax.psum_scatter(
        jnp.dot(context, o_weight, preferred_element_type=jnp.float32).astype(jnp.bfloat16),
        "seq",
        scatter_dimension=0,
        tiled=True,
    )
    row_scale = peer_count * source_rows / loss_total
    own_mask = lax.dynamic_slice_in_dim(slot_info[3], seq_index * part_rows, part_rows, 0).astype(
        jnp.float32
    )
    return (mixed, own_mask * row_scale)


def solution(mesh):
    return jax.shard_map(
        per_device,
        mesh=mesh,
        in_specs=(
            P("dp", None),
            P(None, "dp"),
            P("dp"),
            P(),
            P("dp"),
            P(),
            P(None, "seq"),
            P(None, "seq"),
            P(None, "seq"),
            P("seq"),
            P("seq"),
            P("seq"),
            P("seq", None),
        ),
        out_specs=(P(("dp", "seq"), None), P(("dp", "seq"))),
        check_vma=False,
    )
```

profile of v0, /device:TPU:0, one launch (start us, length us, event | category | flops | bytes accessed | tf_op | source)
XLA Modules:
  0.0 176.1 jit_solution(11099056291222046183)
XLA Ops:
  7.2 0.8 broadcast_in_dim.220
  8.0 0.7 add_select_fusion.1
  8.7 1.4 reduce-window.6
  10.2 0.1 copy.65
  10.3 0.2 reduce-window.9
  10.7 0.7 compare_select_fusion.2
  11.4 4.1 %scatter_custom_fusion = s32[768]{0:T(1024)S(1)} fusion(s32[576]{0:T(1024)S(1)} %get-tuple-element.13, s32[576]{0:T(1024)S(1)} %ne.22, s32[]{:T(128)} %constant.26.clone.1), kind=kCustom, calls=%fused_computation.110 | custom fusion | bytes 3076 | tf_op jit(solution)/shard_map/scatter | solution.py:154
  15.5 4.1 %scatter_custom_fusion.1 = s32[768]{0:T(1024)S(1)} fusion(s32[576]{0:T(1024)S(1)} %get-tuple-element.13, s32[576]{0:T(1024)S(1)} %iota.74, s32[]{:T(128)} %constant.26.clone.1), kind=kCustom, calls=%fused_computation.107 | custom fusion | bytes 3076 | tf_op jit(solution)/shard_map/scatter | solution.py:153
  19.7 0.7 pad_add_fusion
  20.4 0.2 copy.67
  20.6 1.6 gather_fusion
  22.2 0.2 copy.68
  22.4 0.7 fusion.55
  23.1 0.7 reshape.820
  23.8 7.3 %all-to-all-start = ((s32[8,1,480]{2,1,0:T(1,128)}), s32[8,1,480]{2,1,0:T(1,128)S(1)}, u32[]{:S(2)}, u32[]{:S(2)}) async-start(s32[8,1,480]{2,1,0:T(1,128)} %reshape.820), calls=%async_computation | async-start | bytes 32768 | tf_op jit(solution)/shard_map/all_to_all | solution.py:159
  31.1 0.9 slice_reduce_fusion.3
  32.0 3.3 %fusion = f32[576]{0:T(1024)S(1)} fusion(bf16[576,3584]{1,0:T(8,128)(2,1)} %param.14), kind=kLoop, calls=%fused_computation.12 | loop fusion | flops 6192576 | bytes 4131072 | tf_op jit(solution)/shard_map/reduce_sum | solution.py:18
  35.4 1.3 fusion.14
  36.7 1.9 %gather_fusion.1 = bf16[768,128]{1,0:T(8,128)(2,1)S(1)} fusion(bf16[576,128]{1,0:T(8,128)(2,1)S(1)} %fusion.14, s32[1024]{0:T(1024)S(1)} %pad_clamp_fusion), kind=kCustom, calls=%fused_computation.1 | custom fusion | bytes 396288 | tf_op jit(solution)/shard_map/gather | solution.py:172
  38.6 3.5 %fusion.17 = f32[576,1,128]{2,0,1:T(8,128)S(1)} fusion(bf16[3584,128]{1,0:T(8,128)(2,1)S(1)} %copy-done.10, f32[128]{0:T(128)S(1)} %copy-done.14, bf16[576,3584]{1,0:T(8,128)(2,1)} %param.14, f32[3584]{0:T(1024)S(1)} %copy-done.11, f32[576]{0:T(1024)S(1)} %add_rsqrt_fusion), kind=kOutput, calls=%fused_computation.43 | convolution fusion | flops 536961024 | bytes 5358336 | tf_op jit(solution)/shard_map/dot_general | solution.py:58
  42.1 1.6 fusion.32
  43.9 1.9 %gather_fusion.2 = bf16[768,128]{1,0:T(8,128)(2,1)S(1)} fusion(bf16[576,128]{1,0:T(8,128)(2,1)S(1)} %pad_maximum_fusion.1, s32[1024]{0:T(1024)S(1)} %pad_clamp_fusion), kind=kCustom, calls=%fused_computation.2 | custom fusion | bytes 396288 | tf_op jit(solution)/shard_map/gather | solution.py:172
  45.8 5.6 %fusion.7 = f32[576,512]{1,0:T(8,128)S(1)} fusion(bf16[3584,512]{1,0:T(8,128)(2,1)} %param.20, f32[512]{0:T(512)S(1)} %copy-done.12, bf16[576,3584]{1,0:T(8,128)(2,1)} %param.14, f32[3584]{0:T(1024)S(1)} %copy-done.11, f32[576]{0:T(1024)S(1)} %add_rsqrt_fusion), kind=kOutput, calls=%fused_computation.27 | convolution fusion | flops 2123071488 | bytes 8997120 | tf_op jit(solution)/shard_map/dot_general | solution.py:55
  51.4 0.9 broadcast_select_fusion.1
  52.4 6.0 %all-to-all-start.2 = ((bf16[8,96,128]{2,1,0:T(8,128)(2,1)}), bf16[8,96,128]{2,1,0:T(8,128)(2,1)}, u32[]{:S(2)}, u32[]{:S(2)}) async-start(bf16[8,96,128]{2,1,0:T(8,128)(2,1)} %get-tuple-element.15), calls=%async_computation.2 | async-start | bytes 393216 | tf_op jit(solution)/shard_map/all_to_all | solution.py:178
  58.4 2.4 %fusion.27 = (f32[576,64]{1,0:T(8,128)}, f32[576,64]{1,0:T(8,128)}) fusion(f32[64]{0:T(128)S(1)} %multiply_exponential_fusion, s32[576]{0:T(1024)S(1)} %get-tuple-element.3, s32[576]{0:T(1024)S(1)} %get-tuple-element.4, s32[576]{0:T(1024)S(1)} %get-tuple-element.2, pred[64]{0:T(512)(128)(4,1)S(1)} %get-tuple-element.21, pred[64]{0:T(512)(128)(4,1)S(1)} %get-tuple-element.22), kind=kLoop, calls=%fused_computation.59 | loop fusion | flops 147456 | bytes 302208 | tf_op jit(solution)/shard_map/cos | solution.py:36
  60.8 0.4 reshape.703
  61.2 1.9 %subtract_convert_fusion = (bf16[576,4,64]{2,1,0:T(4,128)(2,1)S(1)}, bf16[576,4,64]{2,1,0:T(4,128)(2,1)S(1)}) fusion(f32[576,4,128]{2,1,0:T(4,128)S(1)} %reshape.703, f32[576,64]{1,0:T(8,128)} %get-tuple-element.12, f32[576,64]{1,0:T(8,128)} %get-tuple-element.11), kind=kLoop, calls=%fused_computation.37 | loop fusion | flops 1179648 | bytes 2064384 | tf_op jit(solution)/shard_map/convert.5
  63.1 3.2 %all-to-all-done.2 = bf16[8,96,128]{2,1,0:T(8,128)(2,1)} async-done(((bf16[8,96,128]{2,1,0:T(8,128)(2,1)}), bf16[8,96,128]{2,1,0:T(8,128)(2,1)}, u32[]{:S(2)}, u32[]{:S(2)}) %all-to-all-start.2) | async-done | bytes 196640 | tf_op jit(solution)/shard_map/all_to_all | solution.py:178
  66.3 3.4 %all-to-all-start.1 = ((bf16[8,96,128]{2,1,0:T(8,128)(2,1)}), bf16[8,96,128]{2,1,0:T(8,128)(2,1)S(1)}, u32[]{:S(2)}, u32[]{:S(2)}) async-start(bf16[8,96,128]{2,1,0:T(8,128)(2,1)} %get-tuple-element.16), calls=%async_computation.1 | async-start | bytes 393216 | tf_op jit(solution)/shard_map/all_to_all | solution.py:179
  69.7 0.8 pad_maximum_fusion
  70.6 2.7 %gather_fusion.3 = bf16[768,512]{1,0:T(8,128)(2,1)S(1)} fusion(bf16[576,512]{1,0:T(8,128)(2,1)S(1)} %bitcast.115, s32[1024]{0:T(1024)S(1)} %pad_clamp_fusion), kind=kCustom, calls=%fused_computation.3 | custom fusion | bytes 1575936 | tf_op jit(solution)/shard_map/gather | solution.py:172
  73.3 1.1 broadcast_select_fusion
  74.3 3.1 %all-to-all-done.1 = bf16[8,96,128]{2,1,0:T(8,128)(2,1)S(1)} async-done(((bf16[8,96,128]{2,1,0:T(8,128)(2,1)}), bf16[8,96,128]{2,1,0:T(8,128)(2,1)S(1)}, u32[]{:S(2)}, u32[]{:S(2)}) %all-to-all-start.1) | async-done | bytes 196640 | tf_op jit(solution)/shard_map/all_to_all | solution.py:179
  77.4 3.5 %all-to-all-start.3 = ((bf16[8,96,512]{2,1,0:T(8,128)(2,1)}), bf16[8,96,512]{2,1,0:T(8,128)(2,1)S(1)}, u32[]{:S(2)}, u32[]{:S(2)}) async-start(bf16[8,96,512]{2,1,0:T(8,128)(2,1)} %broadcast_select_fusion), calls=%async_computation.3 | async-start | bytes 1572864 | tf_op jit(solution)/shard_map/all_to_all | solution.py:177
  81.1 0.5 slice.69
  81.6 0.6 iota_compare_fusion.5
  82.6 0.1 broadcast_and_fusion
  82.7 0.5 broadcast.433
  83.3 0.7 reduce.20
  84.1 4.6 %scatter_custom_fusion.3 = bf16[768,128]{1,0:T(8,128)(2,1)S(1)} fusion(s32[768]{0:T(1024)S(1)} %fusion.42, bf16[768,128]{1,0:T(8,128)(2,1)} %bitcast.15, bf16[]{:T(256)} %constant.28.clone.1), kind=kCustom, calls=%fused_computation.78 | custom fusion | bytes 197120 | tf_op jit(solution)/shard_map/scatter | solution.py:81
  88.8 4.3 %scatter_custom_fusion.2 = bf16[768,128]{1,0:T(8,128)(2,1)S(1)} fusion(s32[768]{0:T(1024)S(1)} %fusion.42, bf16[768,128]{1,0:T(8,128)(2,1)S(1)} %bitcast.127, bf16[]{:T(256)} %constant.28.clone.1), kind=kCustom, calls=%fused_computation.80 | custom fusion | bytes 196610 | tf_op jit(solution)/shard_map/scatter | solution.py:81
  93.1 0.6 slice.109
  93.7 0.6 slice.110
  94.4 4.0 %all-to-all-done.3 = bf16[8,96,512]{2,1,0:T(8,128)(2,1)S(1)} async-done(((bf16[8,96,512]{2,1,0:T(8,128)(2,1)}), bf16[8,96,512]{2,1,0:T(8,128)(2,1)S(1)}, u32[]{:S(2)}, u32[]{:S(2)}) %all-to-all-start.3) | async-done | bytes 786464 | tf_op jit(solution)/shard_map/all_to_all | solution.py:177
  98.3 6.2 %scatter_custom_fusion.4 = bf16[768,512]{1,0:T(8,128)(2,1)S(1)} fusion(s32[768]{0:T(1024)S(1)} %fusion.42, bf16[768,512]{1,0:T(8,128)(2,1)S(1)} %bitcast.120, bf16[]{:T(256)} %constant.28.clone.1), kind=kCustom, calls=%fused_computation.55 | custom fusion | bytes 786434 | tf_op jit(solution)/shard_map/scatter | solution.py:81
  104.6 0.2 copy.69
  104.9 1.4 fusion.54
  106.3 0.3 fusion.5
  106.6 0.5 fusion.12
  107.1 0.3 copy.75
  107.5 0.5 fusion.4
  108.0 0.5 fusion.3
  108.6 0.9 fusion.9
  109.5 0.2 copy.76
  109.7 7.4 %convolution_convert_fusion = bf16[768,3584]{1,0:T(8,128)(2,1)} fusion(bf16[512,3584]{1,0:T(8,128)(2,1)} %param.26, bf16[384,512]{1,0:T(8,128)(2,1)S(1)} %bitcast.125, bf16[384,512]{1,0:T(8,128)(2,1)S(1)} %copy.76), kind=kOutput, calls=%fused_computation.15 | convolution fusion | flops 2822897664 | bytes 9961472 | tf_op jit(solution)/shard_map/dot_general | solution.py:188
  117.1 0.7 copy-done.3
  117.7 0.6 reduce_sum.49
  119.0 19.9 %psum.7 = f32[]{:T(128)} all-reduce(f32[]{:T(128)S(6)} %convert_element_type.103), channel_id=1, replica_groups=mesh['dp'=8,'seq'=4] {'dp'}, use_global_device_ids=true, to_apply=%region_16.17 | all-reduce | flops 1 | bytes 8 | tf_op jit(solution)/shard_map/psum | solution.py:160
  139.7 0.2 copy.78
  139.9 4.4 %scatter_custom_fusion.5 = s32[4,768]{0,1:T(8,128)S(1)} fusion(s32[768]{0:T(1024)} %copy-done.4, s32[768,4]{1,0:T(8,128)S(1)} %copy.78, s32[]{:T(128)} %constant.26.clone.1), kind=kCustom, calls=%fused_computation.65 | custom fusion | bytes 12800 | tf_op jit(solution)/shard_map/scatter | solution.py:163
  144.3 0.2 slice.113
  144.4 0.7 multiply_reduce_fusion
  145.1 24.1 %reduce-scatter.2.cloned.1.call-done = bf16[192,3584]{1,0:T(8,128)(2,1)} async-done(((bf16[768,3584]{1,0:T(8,128)(2,1)}), bf16[192,3584]{1,0:T(8,128)(2,1)}) %reduce-scatter.2.cloned.1.call-update) | async-done | bytes 1376272 | tf_op jit(solution)/shard_map/reduce_scatter | solution.py:187
  (65 shorter events, 1.6 us)
Async XLA Ops:
  7.2 28.2 %copy-start = (bf16[3584,128]{1,0:T(8,128)(2,1)S(1)}, bf16[3584,128]{1,0:T(8,128)(2,1)}, u32[]{:S(2)}) copy-start(bf16[3584,128]{1,0:T(8,128)(2,1)} %param.22) | copy-start | bytes 2752516
  22.2 13.1 %copy-start.11 = (f32[3584]{0:T(1024)S(1)}, f32[3584]{0:T(1024)}, u32[]{:S(2)}) copy-start(f32[3584]{0:T(1024)} %param.19) | copy-start | bytes 43012
  22.2 13.1 %copy-start.13 = (f32[128]{0:T(128)S(1)}, f32[128]{0:T(128)}, u32[]{:S(2)}) copy-start(f32[128]{0:T(128)} %param.25) | copy-start | bytes 1540
  23.8 28.6 %all-to-all-start = ((s32[8,1,480]{2,1,0:T(1,128)}), s32[8,1,480]{2,1,0:T(1,128)S(1)}, u32[]{:S(2)}, u32[]{:S(2)}) async-start(s32[8,1,480]{2,1,0:T(1,128)} %reshape.820), calls=%async_computation | async-start | bytes 32768 | tf_op jit(solution)/shard_map/all_to_all | solution.py:159
  31.1 4.3 %copy-start.1 = (bf16[576,3584]{1,0:T(8,128)(2,1)S(1)}, bf16[576,3584]{1,0:T(8,128)(2,1)}, u32[]{:S(2)}) copy-start(bf16[576,3584]{1,0:T(8,128)(2,1)} %param.14) | copy-start | bytes 12386308
  35.4 3.2 %copy-start.10 = (bf16[3584,128]{1,0:T(8,128)(2,1)S(1)}, bf16[3584,128]{1,0:T(8,128)(2,1)}, u32[]{:S(2)}) copy-start(bf16[3584,128]{1,0:T(8,128)(2,1)} %param.21) | copy-start | bytes 2752516
  35.4 3.2 %copy-start.14 = (f32[128]{0:T(128)S(1)}, f32[128]{0:T(128)}, u32[]{:S(2)}) copy-start(f32[128]{0:T(128)} %param.24) | copy-start | bytes 1540
  42.1 3.7 %copy-start.12 = (f32[512]{0:T(512)S(1)}, f32[512]{0:T(512)}, u32[]{:S(2)}) copy-start(f32[512]{0:T(512)} %param.23) | copy-start | bytes 6148
  52.4 13.9 %all-to-all-start.2 = ((bf16[8,96,128]{2,1,0:T(8,128)(2,1)}), bf16[8,96,128]{2,1,0:T(8,128)(2,1)}, u32[]{:S(2)}, u32[]{:S(2)}) async-start(bf16[8,96,128]{2,1,0:T(8,128)(2,1)} %get-tuple-element.15), calls=%async_computation.2 | async-start | bytes 393216 | tf_op jit(solution)/shard_map/all_to_all | solution.py:178
  66.3 11.1 %all-to-all-start.1 = ((bf16[8,96,128]{2,1,0:T(8,128)(2,1)}), bf16[8,96,128]{2,1,0:T(8,128)(2,1)S(1)}, u32[]{:S(2)}, u32[]{:S(2)}) async-start(bf16[8,96,128]{2,1,0:T(8,128)(2,1)} %get-tuple-element.16), calls=%async_computation.1 | async-start | bytes 393216 | tf_op jit(solution)/shard_map/all_to_all | solution.py:179
  73.3 7.7 %copy-start.5 = (s32[8,3]{0,1:T(4,128)S(1)}, s32[8,3]{0,1:T(4,128)}, u32[]{:S(2)}) copy-start(s32[8,3]{0,1:T(4,128)} %param.17) | copy-start | bytes 292
  77.4 21.0 %all-to-all-start.3 = ((bf16[8,96,512]{2,1,0:T(8,128)(2,1)}), bf16[8,96,512]{2,1,0:T(8,128)(2,1)S(1)}, u32[]{:S(2)}, u32[]{:S(2)}) async-start(bf16[8,96,512]{2,1,0:T(8,128)(2,1)} %broadcast_select_fusion), calls=%async_computation.3 | async-start | bytes 1572864 | tf_op jit(solution)/shard_map/all_to_all | solution.py:177
  80.9 88.3 %reduce-scatter.2.cloned.1.call-start = ((), (), s32[]{:S(2)}) async-start(), calls=%async_computation.5 | async-start | bytes 6881280 | tf_op jit(solution)/shard_map/reduce_scatter | solution.py:187
  82.2 6.6 %copy-start.8 = (pred[384]{0:T(512)(128)(4,1)}, pred[384]{0:T(512)(128)(4,1)S(1)}, u32[]{:S(2)}) copy-start(pred[384]{0:T(512)(128)(4,1)S(1)} %iota_compare_fusion.5) | copy-start | bytes 1156
  82.5 6.3 %copy-start.6 = (pred[2,192]{1,0:T(4,128)(4,1)}, pred[2,192]{1,0:T(4,128)(4,1)S(1)}, u32[]{:S(2)}) copy-start(pred[2,192]{1,0:T(4,128)(4,1)S(1)} %iota_compare_fusion.4) | copy-start | bytes 1156
  84.1 14.2 %copy-start.4 = (s32[768]{0:T(1024)}, s32[768]{0:T(1024)S(1)}, u32[]{:S(2)}) copy-start(s32[768]{0:T(1024)S(1)} %fusion.42) | copy-start | bytes 9220
  104.8 1.7 copy-start.2
  104.8 1.7 copy-start.7
  107.5 1.1 copy-start.9
  117.0 0.7 copy-start.3
Sparse Core Ops, SparseCore 0:
  117.2 52.0 reduce-scatter.1
where the time goes:
time: 177 us; the launch traced here: 176 us
  local copies, waits for them, and re-layouts  44 us (25%)
  waiting for transfers between devices  34.3 us (19%)
  matrix products  21.1 us (12%)
  other arithmetic  20.5 us (12%)
  starting transfers between devices  20.3 us (11%)
  blocking collectives  19.9 us (11%)
  between operations  15.9 us (9%)
    reduce_scatter x1, waiting for transfers between devices, per_device(): lax.psum_scatter(jnp.dot(context, o_weight, preferred_element_type=jnp.fl...  24.1 us
    psum x1, blocking collectives, per_device(): loss_total = lax.psum(mask_sum.astype(jnp.float32), 'dp')  19.9 us
    scatter x3, local copies, waits for them, and re-layouts, place_rows(): return empty.at[target_slots].set(flat_rows, mode='drop')  15.1 us
    dot_general x1, matrix products, per_device(): jnp.dot(context, o_weight, preferred_element_type=jnp.float32)  7.37 us
    all_to_all x1, starting transfers between devices, per_device(): lax.all_to_all(send_info, 'dp', split_axis=1, concat_axis=1, tiled=True)  7.28 us
    gather x3, local copies, waits for them, and re-layouts, select_slots(): source_array[source_of]  6.44 us
    all_to_all x1, starting transfers between devices, per_device(): lax.all_to_all(select_slots(k_all), 'dp', split_axis=0, concat_axis=0, ti...  5.99 us
    dot_general x1, matrix products, project(): jnp.dot(normed, q_weight, preferred_element_type=jnp.float32) + q_bias  5.63 us
  transfers between devices with their start and end apart: 5, of which 4 were waited for; matrix products, arithmetic and copies ran while one was open for 28% of the time, Pallas kernels for 0%

commit v1 on v0

v1 whole, which is shorter than its diff:
```python
import math

import jax
import jax.numpy as jnp
from jax import lax
from jax.experimental import pallas as pl
from jax.experimental.pallas import tpu as pltpu
from jax.sharding import PartitionSpec as P

DH = 128
BUCKET = 384
NORM_EPSILON = 1e-06
ROPE_BASE = 1000000.0
META = 128
RADIX = 128


def rotary_tables(position_ids, head_size):
    half_size = head_size // 2
    lane = jnp.arange(head_size, dtype=jnp.int32)
    pair_index = lane % half_size
    inv_freq = jnp.exp(pair_index.astype(jnp.float32) * (-2.0 * math.log(ROPE_BASE) / head_size))
    time_limit = head_size // 8
    height_limit = time_limit + 3 * head_size // 16
    chosen = jnp.where(
        pair_index[None, :] < time_limit,
        position_ids[0][:, None],
        jnp.where(
            pair_index[None, :] < height_limit, position_ids[1][:, None], position_ids[2][:, None]
        ),
    )
    angles = chosen.astype(jnp.float32) * inv_freq[None, :]
    sign = jnp.where(lane < half_size, -1.0, 1.0)
    return jnp.cos(angles), jnp.sin(angles) * sign[None, :]


def chunk_of(width, limit):
    return max(c for c in range(128, limit + 1, 128) if width % c == 0)


def send_kernel(capacity, width, x_ref, gain_ref, wq_ref, wk_ref, wv_ref, bias_ref, cos_ref, sin_ref,
                peer_row_ref, peer_col_ref, meta_ref, out_ref, acc_ref, sq_ref, sel_ref):
    step = pl.program_id(0)
    rows = x_ref.shape[0]
    q_cols, k_cols = wq_ref.shape[1], wk_ref.shape[1]
    slots = out_ref.shape[0]

    @pl.when(step == 0)
    def _():
        acc_ref[...] = jnp.zeros_like(acc_ref)
        sq_ref[...] = jnp.zeros_like(sq_ref)
        peer_row = peer_row_ref[...]
        first = lax.broadcasted_iota(jnp.int32, (rows, rows), 0)
        second = lax.broadcasted_iota(jnp.int32, (rows, rows), 1)
        before = (peer_col_ref[...] == peer_row) & (first < second)
        ranking = jnp.sum(jnp.where(before, 1, 0), axis=0, keepdims=True)
        buffer_slot = peer_row * capacity + ranking
        place = lax.broadcasted_iota(jnp.int32, (slots, rows), 0)
        sel_ref[...] = jnp.where(place == buffer_slot, 1.0, 0.0).astype(jnp.bfloat16)

    wide = x_ref[...].astype(jnp.float32)
    square = wide * wide
    total = sq_ref[...]
    for c in range(0, wide.shape[1], 128):
        total = total + square[:, c : c + 128]
    sq_ref[...] = total
    scaled = (wide * gain_ref[...]).astype(jnp.bfloat16)
    acc_ref[:, :q_cols] += jnp.dot(scaled, wq_ref[...], preferred_element_type=jnp.float32)
    acc_ref[:, q_cols : q_cols + k_cols] += jnp.dot(
        scaled, wk_ref[...], preferred_element_type=jnp.float32
    )
    acc_ref[:, q_cols + k_cols :] += jnp.dot(
        scaled, wv_ref[...], preferred_element_type=jnp.float32
    )

    @pl.when(step == pl.num_programs(0) - 1)
    def _():
        mean_square = jnp.sum(sq_ref[...], axis=1, keepdims=True) * (1.0 / width)
        inverse = lax.rsqrt(mean_square + NORM_EPSILON)
        cosine, sine = cos_ref[...], sin_ref[...]
        pick = sel_ref[...]
        for c in range(0, acc_ref.shape[1], DH):
            head = acc_ref[:, c : c + DH] * inverse + bias_ref[:, c : c + DH]
            head = head.astype(jnp.bfloat16)
            if c < q_cols + k_cols:
                head = head.astype(jnp.float32)
                head = (head * cosine + pltpu.roll(head, DH // 2, 1) * sine).astype(jnp.bfloat16)
            acc_ref[:, c : c + DH] = head.astype(jnp.float32)
        every = acc_ref[...].astype(jnp.bfloat16)
        cols = acc_ref.shape[1]
        out_ref[:, :cols] = jnp.dot(pick, every, preferred_element_type=jnp.float32).astype(
            jnp.bfloat16
        )
        meta = meta_ref[...]
        moved = jnp.dot(pick, meta, preferred_element_type=jnp.float32)
        column_sum = jnp.sum(meta.astype(jnp.float32), axis=0, keepdims=True)
        high = jnp.floor(column_sum * (1.0 / RADIX))
        lane = lax.broadcasted_iota(jnp.int32, (1, META), 1)
        digits = jnp.where(lane == 3, high, jnp.where(lane == 4, column_sum - RADIX * high, 0.0))
        row = lax.broadcasted_iota(jnp.int32, (slots, META), 0)
        leads = row % capacity == 0
        moved = jnp.where(lane >= 3, jnp.where(leads, digits, 0.0), moved)
        out_ref[:, cols:] = moved.astype(jnp.bfloat16)


def attend_kernel(total_rows, kv_count, group_size, lengths_ref, recv_ref, out_ref, weight_ref,
                  place_ref):
    slots = recv_ref.shape[0]
    q_cols = kv_count * group_size * DH
    cols = q_cols + 2 * kv_count * DH
    meta = recv_ref[:, cols:]
    row = lax.broadcasted_iota(jnp.int32, (8, META), 0)
    lane = lax.broadcasted_iota(jnp.int32, (8, META), 1)
    high = ((row == 0) & (lane == 0)) | ((row == 2) & (lane == 3))
    low = ((row == 0) & (lane == 1)) | ((row == 1) & (lane == 2)) | ((row == 2) & (lane == 4))
    decode = jnp.where(high, float(RADIX), jnp.where(low, 1.0, 0.0)).astype(jnp.bfloat16)
    across = (((1,), (1,)), ((), ()))
    facts = lax.dot_general(decode, meta, across, preferred_element_type=jnp.float32)
    slot_row = facts[0:1].astype(jnp.int32) - 1
    place = lax.broadcasted_iota(jnp.int32, (slots, slots), 0)
    chosen = jnp.where(place == slot_row, 1.0, 0.0).astype(jnp.bfloat16)
    place_ref[...] = jnp.dot(
        chosen, recv_ref[:, :cols], preferred_element_type=jnp.float32
    ).astype(jnp.bfloat16)
    flags = lax.dot_general(
        facts.astype(jnp.bfloat16), chosen, across, preferred_element_type=jnp.float32
    )
    count = jnp.sum(facts[2:3], axis=1, keepdims=True)
    weight_ref[...] = flags[1:2] * (total_rows / count)
    block = BUCKET // 2
    for bucket, start, size in ((0, 0, BUCKET), (1, BUCKET, block), (2, BUCKET + block, block)):
        length = lengths_ref[bucket]
        for first in range(0, size, block):
            keys = first + block
            places = first + lax.broadcasted_iota(jnp.int32, (block, keys), 0)
            others = lax.broadcasted_iota(jnp.int32, (block, keys), 1)
            allowed = (places >= others) & (others < length)
            live = first + lax.broadcasted_iota(jnp.int32, (block, DH), 0) < length
            for g in range(kv_count):
                k_at = q_cols + g * DH
                v_at = k_at + kv_count * DH
                k_rows = place_ref[start : start + keys, k_at : k_at + DH]
                v_rows = place_ref[start : start + keys, v_at : v_at + DH]
                for h in range(g * group_size, (g + 1) * group_size):
                    own = slice(start + first, start + first + block)
                    head = slice(h * DH, (h + 1) * DH)
                    scores = lax.dot_general(
                        place_ref[own, head], k_rows, across, preferred_element_type=jnp.float32
                    ) * (1.0 / math.sqrt(DH))
                    scores = jnp.where(allowed, scores, -1e30)
                    top = jnp.max(scores, axis=1, keepdims=True)
                    grown = jnp.exp(scores - top)
                    share = 1.0 / jnp.sum(grown, axis=1, keepdims=True)
                    probs = (grown * share).astype(jnp.bfloat16)
                    context = jnp.dot(probs, v_rows, preferred_element_type=jnp.float32)
                    out_ref[own, head] = jnp.where(live, context, 0.0).astype(jnp.bfloat16)


def sum_groups(context, o_weight, seq_count, seq_index):
    def product(rows):
        return jnp.dot(rows, o_weight, preferred_element_type=jnp.float32).astype(jnp.bfloat16)

    if seq_count != 4:
        return lax.psum_scatter(product(context), "seq", scatter_dimension=0, tiled=True)
    near = [(i, i ^ 1) for i in range(seq_count)]
    far = [(i, i ^ 2) for i in range(seq_count)]
    parts = context.reshape(seq_count, -1, context.shape[1])

    def part(which):
        return lax.dynamic_index_in_dim(parts, which, 0, keepdims=False)

    def widened(array):
        return array.astype(jnp.float32)

    from_near = lax.ppermute(product(part(seq_index ^ 3)), "seq", near)
    for_far = product(part(seq_index ^ 2))
    from_far = lax.ppermute((widened(for_far) + widened(from_near)).astype(jnp.bfloat16), "seq", far)
    own_near = lax.ppermute(product(part(seq_index ^ 1)), "seq", near)
    own = product(part(seq_index))
    return (widened(own) + widened(own_near) + widened(from_far)).astype(jnp.bfloat16)


def per_device(tokens, positions, loss_mask, sample_tokens, dest_slot, norm_gain, q_weight, k_weight,
               v_weight, q_bias, k_bias, v_bias, o_weight):
    peer_count = lax.axis_size("dp")
    seq_count = lax.axis_size("seq")
    own_index = lax.axis_index("dp")
    seq_index = lax.axis_index("seq")
    rows, width = tokens.shape
    slots = 2 * BUCKET
    capacity = slots // peer_count
    q_cols, k_cols, v_cols = q_weight.shape[1], k_weight.shape[1], v_weight.shape[1]
    kv_count = k_cols // DH
    group_size = q_cols // k_cols
    cols = q_cols + k_cols + v_cols
    peer = dest_slot // slots
    code = dest_slot % slots + 1
    lane = jnp.arange(META, dtype=jnp.int32)[None, :]
    meta = jnp.where(
        lane == 0,
        (code // RADIX)[:, None],
        jnp.where(lane == 1, (code % RADIX)[:, None], jnp.where(lane < 5, loss_mask[:, None], 0)),
    ).astype(jnp.bfloat16)
    cosine, sine = rotary_tables(positions, DH)
    bias = jnp.concatenate([q_bias, k_bias, v_bias])[None, :]
    chunk = chunk_of(width, 512)
    whole = lambda *shape: pl.BlockSpec(shape, lambda i: (0, 0))
    down = lambda n: pl.BlockSpec((chunk, n), lambda i: (i, 0))
    across = lambda n: pl.BlockSpec((n, chunk), lambda i: (0, i))
    send = pl.pallas_call(
        lambda *refs: send_kernel(capacity, width, *refs),
        name="project_and_pack",
        grid=(width // chunk,),
        in_specs=[across(rows), across(1), down(q_cols), down(k_cols), down(v_cols), whole(1, cols),
                  whole(rows, DH), whole(rows, DH), whole(1, rows), whole(rows, 1),
                  whole(rows, META)],
        out_specs=whole(slots, cols + META),
        out_shape=jax.ShapeDtypeStruct((slots, cols + META), jnp.bfloat16),
        scratch_shapes=[pltpu.VMEM((rows, cols), jnp.float32), pltpu.VMEM((rows, 128), jnp.float32),
                        pltpu.VMEM((slots, rows), jnp.bfloat16)],
    )(tokens, norm_gain[None, :], q_weight, k_weight, v_weight, bias, cosine, sine, peer[None, :],
      peer[:, None], meta)
    recv = lax.all_to_all(
        send.reshape(peer_count, capacity, cols + META), "dp", split_axis=0, concat_axis=0, tiled=True
    ).reshape(slots, cols + META)
    lengths = sample_tokens[own_index]
    context, weights = pl.pallas_call(
        lambda *refs: attend_kernel(float(peer_count * rows), kv_count, group_size, *refs),
        name="place_and_attend",
        in_specs=[pl.BlockSpec(memory_space=pltpu.SMEM), pl.BlockSpec(memory_space=pltpu.VMEM)],
        out_specs=[pl.BlockSpec(memory_space=pltpu.VMEM), pl.BlockSpec(memory_space=pltpu.VMEM)],
        out_shape=[jax.ShapeDtypeStruct((slots, q_cols), jnp.bfloat16),
                   jax.ShapeDtypeStruct((1, slots), jnp.float32)],
        scratch_shapes=[pltpu.VMEM((slots, cols), jnp.bfloat16)],
    )(lengths, recv)
    part_rows = slots // seq_count
    own_weights = lax.dynamic_slice_in_dim(weights[0], seq_index * part_rows, part_rows, 0)
    return sum_groups(context, o_weight, seq_count, seq_index), own_weights


def solution(mesh):
    return jax.shard_map(
        per_device,
        mesh=mesh,
        in_specs=(P("dp", None), P(None, "dp"), P("dp"), P(), P("dp"), P(), P(None, "seq"),
                  P(None, "seq"), P(None, "seq"), P("seq"), P("seq"), P("seq"), P("seq", None)),
        out_specs=(P(("dp", "seq"), None), P(("dp", "seq"))),
        check_vma=False,
    )
```

time: 177 us -> 119 us (0.67)
  local copies, waits for them, and re-layouts: 44 us -> 7.29 us
  waiting for transfers between devices: 34.3 us -> 58.7 us
  blocking collectives: 19.9 us -> 0 us
  Pallas kernels: 0 us -> 19.8 us
  between operations: 15.9 us -> 0.71 us
  other arithmetic: 20.5 us -> 8.48 us
  starting transfers between devices: 20.3 us -> 9.4 us
  matrix products: 21.1 us -> 13.5 us
    scatter x6 -> x0, local copies, waits for them, and re-layouts: 27.7 us -> none  [the longest x3 15.1 us: place_rows(): return empty.at[target_slots].set(flat_rows, mode='drop')]
    ppermute x0 -> x3, waiting for transfers between devices: none -> 26.6 us  [the longest x1 26.6 us: sum_groups(): lax.ppermute((widened(for_far) + widened(from_near)).astype(jnp.bfloat16)...]
    reduce_scatter x1 -> x0, waiting for transfers between devices: 24.1 us -> none  [per_device(): lax.psum_scatter(jnp.dot(context, o_weight, preferred_element_type=jnp.fl...]
    all_to_all x4 -> x1, waiting for transfers between devices: 10.2 us -> 32.1 us  [per_device(): lax.all_to_all(send.reshape(peer_count, capacity, cols + META), 'dp', spl...]
    psum x1 -> x0, blocking collectives: 19.9 us -> none  [per_device(): loss_total = lax.psum(mask_sum.astype(jnp.float32), 'dp')]
    pallas_call x0 -> x2, Pallas kernels: none -> 19.8 us  [the longest x1 12.5 us: per_device(): pl.pallas_call(lambda *refs: send_kernel(capacity, width, *refs), name='p...]
    all_to_all x4 -> x1, starting transfers between devices: 20.2 us -> 7.29 us  [per_device(): lax.all_to_all(send.reshape(peer_count, capacity, cols + META), 'dp', spl...]
    gather x5 -> x0, local copies, waits for them, and re-layouts: 8.17 us -> none  [the longest x3 6.44 us: select_slots(): source_array[source_of]]
  transfers between devices with their start and end apart: 5 -> 4, of which waited for: 4 -> 2; matrix products, arithmetic and copies ran while one was open for 28% -> 10% of each run, Pallas kernels for 0% -> 0%
where the time goes in v1:
time: 119 us; the launch traced here: 118 us
  waiting for transfers between devices  58.7 us (49%)
  Pallas kernels  19.8 us (17%)
  matrix products  13.5 us (11%)
  starting transfers between devices  9.4 us (8%)
  other arithmetic  8.48 us (7%)
  local copies, waits for them, and re-layouts  7.29 us (6%)
    all_to_all x1, waiting for transfers between devices, per_device(): lax.all_to_all(send.reshape(peer_count, capacity, cols + META), 'dp', spl...  32.1 us
    ppermute x1, waiting for transfers between devices, sum_groups(): lax.ppermute((widened(for_far) + widened(from_near)).astype(jnp.bfloat16)...  26.6 us
    dot_general x4, matrix products, product(): jnp.dot(rows, o_weight, preferred_element_type=jnp.float32)  13.5 us
    pallas_call x1, Pallas kernels, per_device(): pl.pallas_call(lambda *refs: send_kernel(capacity, width, *refs), name='p...  12.5 us
    all_to_all x1, starting transfers between devices, per_device(): lax.all_to_all(send.reshape(peer_count, capacity, cols + META), 'dp', spl...  7.29 us
    pallas_call x1, Pallas kernels, per_device(): pl.pallas_call(lambda *refs: attend_kernel(float(peer_count * rows), kv_c...  7.29 us
    convert_element_type x1, other arithmetic, sum_groups(): (widened(own) + widened(own_near) + widened(from_far)).astype(jnp.bfloat16)  2.94 us
    mul x1, other arithmetic, rotary_tables(): return (jnp.cos(angles), jnp.sin(angles) * sign[None, :])  2.43 us
  transfers between devices with their start and end apart: 4, of which 2 were waited for; matrix products, arithmetic and copies ran while one was open for 10% of the time, Pallas kernels for 0%

profile of v1, /device:TPU:0, one launch (start us, length us, event | category | flops | bytes accessed | tf_op | source)
XLA Modules:
  0.0 117.9 jit_solution(8382069195178457181)
XLA Ops:
  0.6 0.0 copy-start
  0.7 0.7 add_select_fusion.1
  1.4 0.6 broadcast_in_dim.126.refs_8_
  2.0 0.8 broadcast_in_dim.135.refs_9_
  2.8 0.7 pad_maximum_fusion
  3.6 0.6 broadcast_in_dim.115.refs_5_
  4.2 0.8 slice_reduce_fusion.2
  5.0 1.3 %broadcast_in_dim.114.refs_1_ = f32[1,3584]{1,0:T(1,128)} reshape(f32[3584]{0:T(1024)} %param.18) | data formatting | bytes 28672 | tf_op jit(solution)/shard_map/broadcast_in_dim | solution.py:221
  6.3 1.6 %select_convert_fusion.refs_10_ = bf16[576,128]{1,0:T(8,128)(2,1)} fusion(s32[576]{0:T(1024)} %param.15, s32[576]{0:T(1024)S(1)} %get-tuple-element.12, s32[576]{0:T(1024)S(1)} %get-tuple-element.11, pred[128]{0:T(512)(128)(4,1)S(1)} %get-tuple-element.18, pred[128]{0:T(512)(128)(4,1)S(1)} %get-tuple-element.19, pred[128]{0:T(512)(128)(4,1)S(1)} %get-tuple-element.14), kind=kLoop, calls=%fused_computation.8 | loop fusion | flops 294912 | bytes 154752 | tf_op jit(solution)/shard_map/convert_element_type | solution.py:203
  8.0 2.4 %sine_multiply_fusion = (f32[576,128]{1,0:T(8,128)}, f32[576,128]{1,0:T(8,128)}) fusion(f32[128]{0:T(128)S(1)} %get-tuple-element.16, f32[128]{0:T(128)S(1)} %get-tuple-element.17, s32[576]{0:T(1024)S(1)} %get-tuple-element.7, s32[576]{0:T(1024)S(1)} %get-tuple-element.8, s32[576]{0:T(1024)S(1)} %get-tuple-element.6, pred[128]{0:T(512)(128)(4,1)S(1)} %get-tuple-element.15, ...), kind=kLoop, calls=%fused_computation.9 | loop fusion | flops 368640 | bytes 598016 | tf_op jit(solution)/shard_map/mul | solution.py:34
  10.4 12.5 %project_and_pack.1 = bf16[768,896]{1,0:T(8,128)(2,1)} custom-call(bf16[576,3584]{1,0:T(8,128)(2,1)} %refs_0_.1, f32[1,3584]{1,0:T(1,128)} %broadcast_in_dim.114.refs_1_, bf16[3584,512]{1,0:T(8,128)(2,1)} %refs_2_.1, bf16[3584,128]{1,0:T(8,128)(2,1)} %refs_3_.1, bf16[3584,128]{1,0:T(8,128)(2,1)} %refs_4_.1, f32[1,768]{1,0:T(1,128)} %broadcast_in_dim.115.refs_5_, ...), custom_call_target="tpu_custom_call" | custom-call | tf_op jit(solution)/shard_map/project_and_pack/pallas_call | solution.py:210
  22.9 7.3 %all-to-all-start = ((bf16[8,96,896]{2,1,0:T(8,128)(2,1)}), bf16[8,96,896]{2,1,0:T(8,128)(2,1)S(1)}, u32[]{:S(2)}, u32[]{:S(2)}) async-start(bf16[8,96,896]{2,1,0:T(8,128)(2,1)} %bitcast.23), calls=%async_computation | async-start | bytes 2752512 | tf_op jit(solution)/shard_map/all_to_all | solution.py:223
  30.2 0.0 copy-done
  30.2 0.7 dynamic-slice_reduce_fusion.refs_0_
  30.9 32.1 %all-to-all-done = bf16[8,96,896]{2,1,0:T(8,128)(2,1)S(1)} async-done(((bf16[8,96,896]{2,1,0:T(8,128)(2,1)}), bf16[8,96,896]{2,1,0:T(8,128)(2,1)S(1)}, u32[]{:S(2)}, u32[]{:S(2)}) %all-to-all-start) | async-done | bytes 1376288 | tf_op jit(solution)/shard_map/all_to_all | solution.py:223
  62.9 0.0 copy-start.2
  62.9 1.1 copy-done.2
  64.0 7.3 %place_and_attend.1 = (bf16[768,512]{1,0:T(8,128)(2,1)}, f32[1,768]{1,0:T(1,128)}) custom-call(s32[3]{0:T(128)} %dynamic-slice_reduce_fusion.refs_0_, bf16[768,896]{1,0:T(8,128)(2,1)} %bitcast.22), custom_call_target="tpu_custom_call" | custom-call | tf_op jit(solution)/shard_map/place_and_attend/pallas_call | solution.py:227
  71.3 0.0 copy-start.3
  71.3 4.2 %convolution_convert_fusion = bf16[192,3584]{1,0:T(8,128)(2,1)} fusion(bf16[512,3584]{1,0:T(8,128)(2,1)} %param.25, bf16[4,192,512]{2,1,0:T(8,128)(2,1)} %bitcast.24, s32[]{:T(128)S(6)} %select_n.99), kind=kOutput, calls=%fused_computation | convolution fusion | flops 705331200 | bytes 5242884 | tf_op jit(solution)/shard_map/dot_general | solution.py:161
  75.5 0.0 collective-permute-start.1
  75.5 0.0 copy-done.3
  75.5 0.0 copy-start.1
  75.5 3.1 %convolution_convert_fusion.2 = bf16[192,3584]{1,0:T(8,128)(2,1)S(1)} fusion(bf16[512,3584]{1,0:T(8,128)(2,1)} %param.25, bf16[4,192,512]{2,1,0:T(8,128)(2,1)S(1)} %bitcast.25, s32[]{:T(128)S(6)} %select_n.97), kind=kOutput, calls=%fused_computation.3 | convolution fusion | flops 705331200 | bytes 5242884 | tf_op jit(solution)/shard_map/dot_general | solution.py:161
  78.6 0.6 collective-permute-start
  79.2 0.0 collective-permute-done.1
  79.2 0.0 copy-done.1
  79.2 3.3 %add_convert_fusion.1 = bf16[192,3584]{1,0:T(8,128)(2,1)} fusion(bf16[192,3584]{1,0:T(8,128)(2,1)} %collective-permute-done.1, bf16[512,3584]{1,0:T(8,128)(2,1)S(1)} %copy-done.1, bf16[4,192,512]{2,1,0:T(8,128)(2,1)S(1)} %bitcast.26, s32[]{:T(128)S(6)} %select_n.98), kind=kOutput, calls=%fused_computation.7 | convolution fusion | flops 708083712 | bytes 6619140 | tf_op jit(solution)/shard_map/dot_general | solution.py:161
  82.5 1.5 %collective-permute-start.2 = (bf16[192,3584]{1,0:T(8,128)(2,1)}, bf16[192,3584]{1,0:T(8,128)(2,1)}, u32[]{:S(2)}, u32[]{:S(2)}) collective-permute-start(bf16[192,3584]{1,0:T(8,128)(2,1)} %add_convert_fusion.1), channel_id=1, source_target_pairs={{0,2},{1,3},{2,0},{3,1},{4,6},{5,7},{6,4},{7,5},{8,10},{9,11},{10,... | collective-permute-start | bytes 4128776 | tf_op jit(solution)/shard_map/ppermute | solution.py:177
  84.1 1.3 %constant_dynamic-slice_fusion = f32[1,192]{1,0:T(1,128)} fusion(f32[1,768]{1,0:T(1,128)} %get-tuple-element.5, s32[]{:T(128)S(6)} %select_n.100), kind=kLoop, calls=%fused_computation.41 | loop fusion | bytes 1540 | tf_op jit(solution)/shard_map/dynamic_slice | solution.py:237
  85.4 2.9 %fusion.1 = f32[192,3584]{1,0:T(8,128)S(1)} fusion(bf16[512,3584]{1,0:T(8,128)(2,1)} %param.25, bf16[4,192,512]{2,1,0:T(8,128)(2,1)S(1)} %bitcast.27, s32[]{:T(128)S(6)} %select_n.96), kind=kOutput, calls=%fused_computation.5 | convolution fusion | flops 706019328 | bytes 6619140 | tf_op jit(solution)/shard_map/dot_general | solution.py:161
  88.3 0.0 collective-permute-done
  88.3 26.6 %collective-permute-done.2 = bf16[192,3584]{1,0:T(8,128)(2,1)} collective-permute-done((bf16[192,3584]{1,0:T(8,128)(2,1)}, bf16[192,3584]{1,0:T(8,128)(2,1)}, u32[]{:S(2)}, u32[]{:S(2)}) %collective-permute-start.2) | collective-permute-done | bytes 1376288 | tf_op jit(solution)/shard_map/ppermute | solution.py:177
  115.0 2.9 %add_convert_fusion = bf16[192,3584]{1,0:T(8,128)(2,1)} fusion(bf16[192,3584]{1,0:T(8,128)(2,1)} %collective-permute-done.2, f32[192,3584]{1,0:T(8,128)S(1)} %fusion.1, bf16[192,3584]{1,0:T(8,128)(2,1)S(1)} %collective-permute-done), kind=kLoop, calls=%fused_computation.6 | loop fusion | flops 3440640 | bytes 6881280 | tf_op jit(solution)/shard_map/convert_element_type | solution.py:180
  (4 shorter events, 0.0 us)
Async XLA Ops:
  0.6 29.5 %copy-start = (s32[8,3]{0,1:T(4,128)S(1)}, s32[8,3]{0,1:T(4,128)}, u32[]{:S(2)}) copy-start(s32[8,3]{0,1:T(4,128)} %param.16) | copy-start | bytes 292
  22.9 40.1 %all-to-all-start = ((bf16[8,96,896]{2,1,0:T(8,128)(2,1)}), bf16[8,96,896]{2,1,0:T(8,128)(2,1)S(1)}, u32[]{:S(2)}, u32[]{:S(2)}) async-start(bf16[8,96,896]{2,1,0:T(8,128)(2,1)} %bitcast.23), calls=%async_computation | async-start | bytes 2752512 | tf_op jit(solution)/shard_map/all_to_all | solution.py:223
  62.9 1.1 copy-start.2
  71.3 4.2 %copy-start.3 = (bf16[768,512]{1,0:T(8,128)(2,1)S(1)}, bf16[768,512]{1,0:T(8,128)(2,1)}, u32[]{:S(2)}) copy-start(bf16[768,512]{1,0:T(8,128)(2,1)} %get-tuple-element.4) | copy-start | bytes 2359300
  75.5 3.7 %collective-permute-start.1 = (bf16[192,3584]{1,0:T(8,128)(2,1)}, bf16[192,3584]{1,0:T(8,128)(2,1)}, u32[]{:S(2)}, u32[]{:S(2)}) collective-permute-start(bf16[192,3584]{1,0:T(8,128)(2,1)} %convolution_convert_fusion), channel_id=1, source_target_pairs={{0,1},{1,0},{2,3},{3,2},{4,5},{5,4},{6,7},{7,6},{8,9},{9,8},{10,11... | collective-permute-start | bytes 4128776 | tf_op jit(solution)/shard_map/ppermute | solution.py:175
  75.5 3.7 %copy-start.1 = (bf16[512,3584]{1,0:T(8,128)(2,1)S(1)}, bf16[512,3584]{1,0:T(8,128)(2,1)}, u32[]{:S(2)}) copy-start(bf16[512,3584]{1,0:T(8,128)(2,1)} %param.25) | copy-start | bytes 11010052
  78.6 9.7 %collective-permute-start = (bf16[192,3584]{1,0:T(8,128)(2,1)S(1)}, bf16[192,3584]{1,0:T(8,128)(2,1)S(1)}, u32[]{:S(2)}, u32[]{:S(2)}) collective-permute-start(bf16[192,3584]{1,0:T(8,128)(2,1)S(1)} %convolution_convert_fusion.2), channel_id=1, source_target_pairs={{0,1},{1,0},{2,3},{3,2},{4,5},{5,4},{6,7},{7,6},{8,9},{9,8},{10,11... | collective-permute-start | bytes 4128776 | tf_op jit(solution)/shard_map/ppermute | solution.py:178
  82.5 32.4 %collective-permute-start.2 = (bf16[192,3584]{1,0:T(8,128)(2,1)}, bf16[192,3584]{1,0:T(8,128)(2,1)}, u32[]{:S(2)}, u32[]{:S(2)}) collective-permute-start(bf16[192,3584]{1,0:T(8,128)(2,1)} %add_convert_fusion.1), channel_id=1, source_target_pairs={{0,2},{1,3},{2,0},{3,1},{4,6},{5,7},{6,4},{7,5},{8,10},{9,11},{10,... | collective-permute-start | bytes 4128776 | tf_op jit(solution)/shard_map/ppermute | solution.py:177

commit v2 on v1

--- a/solution.py
+++ b/solution.py
@@ -15,33 +15,27 @@
 RADIX = 128
 
 
-def rotary_tables(position_ids, head_size):
-    half_size = head_size // 2
-    lane = jnp.arange(head_size, dtype=jnp.int32)
-    pair_index = lane % half_size
-    inv_freq = jnp.exp(pair_index.astype(jnp.float32) * (-2.0 * math.log(ROPE_BASE) / head_size))
-    time_limit = head_size // 8
-    height_limit = time_limit + 3 * head_size // 16
-    chosen = jnp.where(
-        pair_index[None, :] < time_limit,
-        position_ids[0][:, None],
-        jnp.where(
-            pair_index[None, :] < height_limit, position_ids[1][:, None], position_ids[2][:, None]
-        ),
-    )
-    angles = chosen.astype(jnp.float32) * inv_freq[None, :]
-    sign = jnp.where(lane < half_size, -1.0, 1.0)
-    return jnp.cos(angles), jnp.sin(angles) * sign[None, :]
-
-
 def chunk_of(width, limit):
     return max(c for c in range(128, limit + 1, 128) if width % c == 0)
 
 
-def send_kernel(capacity, width, x_ref, gain_ref, wq_ref, wk_ref, wv_ref, bias_ref, cos_ref, sin_ref,
-                peer_row_ref, peer_col_ref, meta_ref, out_ref, acc_ref, sq_ref, sel_ref):
+def column_weights(count):
+    row = lax.broadcasted_iota(jnp.int32, (count, DH), 0)
+    lane = lax.broadcasted_iota(jnp.int32, (count, DH), 1)
+    pair = lane % (DH // 2)
+    time_limit = DH // 8
+    height_limit = time_limit + 3 * DH // 16
+    axis = jnp.where(pair < time_limit, 0, jnp.where(pair < height_limit, 1, 2))
+    ids = jnp.where(row == 2 * axis, float(RADIX), jnp.where(row == 2 * axis + 1, 1.0, 0.0))
+    carried = ((row == 6) & (lane == 0)) | ((row == 7) & (lane == 1))
+    carried = carried | ((row == 8) & (lane >= 2) & (lane < 5))
+    return ids, jnp.where(carried, 1.0, 0.0), jnp.where(row == 9, 1.0, 0.0)
+
+
+def send_kernel(capacity, width, x_ref, gain_ref, wq_ref, wk_ref, wv_ref, bq_ref, bk_ref, bv_ref,
+                info_ref, out_ref, acc_ref, sq_ref, sel_ref, cos_ref, sin_ref, meta_ref):
     step = pl.program_id(0)
-    rows = x_ref.shape[0]
+    rows, chunk = x_ref.shape
     q_cols, k_cols = wq_ref.shape[1], wk_ref.shape[1]
     slots = out_ref.shape[0]
 
@@ -49,22 +43,37 @@
     def _():
         acc_ref[...] = jnp.zeros_like(acc_ref)
         sq_ref[...] = jnp.zeros_like(sq_ref)
-        peer_row = peer_row_ref[...]
+        info = info_ref[...]
+
+        def columns(weights):
+            return lax.dot_general(info, weights.astype(jnp.bfloat16), (((0,), (0,)), ((), ())),
+                                   preferred_element_type=jnp.float32)
+
+        ids, carried, peers = (columns(w) for w in column_weights(info.shape[0]))
+        meta_ref[...] = carried.astype(jnp.bfloat16)
+        lane = lax.broadcasted_iota(jnp.int32, (1, DH), 1)
+        pair = (lane % (DH // 2)).astype(jnp.float32)
+        angles = ids * jnp.exp(pair * (-2.0 * math.log(ROPE_BASE) / DH))
+        cos_ref[...] = jnp.cos(angles)
+        sin_ref[...] = jnp.sin(angles) * jnp.where(lane < DH // 2, -1.0, 1.0)
+        peer_row = info[9:10].astype(jnp.float32)
         first = lax.broadcasted_iota(jnp.int32, (rows, rows), 0)
         second = lax.broadcasted_iota(jnp.int32, (rows, rows), 1)
-        before = (peer_col_ref[...] == peer_row) & (first < second)
-        ranking = jnp.sum(jnp.where(before, 1, 0), axis=0, keepdims=True)
-        buffer_slot = peer_row * capacity + ranking
+        before = (peers[:, :1] == peer_row) & (first < second)
+        ranking = jnp.sum(jnp.where(before, 1.0, 0.0), axis=0, keepdims=True)
+        buffer_slot = (peer_row * capacity + ranking).astype(jnp.int32)
         place = lax.broadcasted_iota(jnp.int32, (slots, rows), 0)
         sel_ref[...] = jnp.where(place == buffer_slot, 1.0, 0.0).astype(jnp.bfloat16)
 
-    wide = x_ref[...].astype(jnp.float32)
-    square = wide * wide
     total = sq_ref[...]
-    for c in range(0, wide.shape[1], 128):
-        total = total + square[:, c : c + 128]
+    pieces = []
+    for c in range(chunk // 128):
+        wide = x_ref[:, c * 128 : (c + 1) * 128].astype(jnp.float32)
+        total = total + wide * wide
+        gain = gain_ref[pl.ds(step * (chunk // 128) + c, 1), :]
+        pieces.append((wide * gain).astype(jnp.bfloat16))
     sq_ref[...] = total
-    scaled = (wide * gain_ref[...]).astype(jnp.bfloat16)
+    scaled = jnp.concatenate(pieces, axis=1)
     acc_ref[:, :q_cols] += jnp.dot(scaled, wq_ref[...], preferred_element_type=jnp.float32)
     acc_ref[:, q_cols : q_cols + k_cols] += jnp.dot(
         scaled, wk_ref[...], preferred_element_type=jnp.float32
@@ -79,8 +88,9 @@
         inverse = lax.rsqrt(mean_square + NORM_EPSILON)
         cosine, sine = cos_ref[...], sin_ref[...]
         pick = sel_ref[...]
+        bias = [r[i : i + 1] for r in (bq_ref, bk_ref, bv_ref) for i in range(r.shape[0])]
         for c in range(0, acc_ref.shape[1], DH):
-            head = acc_ref[:, c : c + DH] * inverse + bias_ref[:, c : c + DH]
+            head = acc_ref[:, c : c + DH] * inverse + bias[c // DH]
             head = head.astype(jnp.bfloat16)
             if c < q_cols + k_cols:
                 head = head.astype(jnp.float32)
@@ -156,28 +166,55 @@
                     out_ref[own, head] = jnp.where(live, context, 0.0).astype(jnp.bfloat16)
 
 
-def sum_groups(context, o_weight, seq_count, seq_index):
-    def product(rows):
-        return jnp.dot(rows, o_weight, preferred_element_type=jnp.float32).astype(jnp.bfloat16)
-
+def early_columns(width):
+    return width * 5 // 7 // 128 * 128
+
+
+def partners(seq_count, bit):
+    return [(i, i ^ bit) for i in range(seq_count)]
+
+
+def product(rows, weight):
+    return jnp.dot(rows, weight, preferred_element_type=jnp.float32)
+
+
+def sum_groups(context, o_weight, far_weight, seq_count, seq_index):
     if seq_count != 4:
-        return lax.psum_scatter(product(context), "seq", scatter_dimension=0, tiled=True)
-    near = [(i, i ^ 1) for i in range(seq_count)]
-    far = [(i, i ^ 2) for i in range(seq_count)]
-    parts = context.reshape(seq_count, -1, context.shape[1])
-
-    def part(which):
+        partial = product(context, o_weight).astype(jnp.bfloat16)
+        return lax.psum_scatter(partial, "seq", scatter_dimension=0, tiled=True)
+    near, far = partners(seq_count, 1), partners(seq_count, 2)
+    early = far_weight.shape[1]
+    head_weight, tail_weight = o_weight[:, :early], o_weight[:, early:]
+    parts = context.reshape(2, 2, -1, context.shape[1])
+    half, core = seq_index // 2, seq_index % 2
+
+    def halves(which):
         return lax.dynamic_index_in_dim(parts, which, 0, keepdims=False)
 
-    def widened(array):
-        return array.astype(jnp.float32)
-
-    from_near = lax.ppermute(product(part(seq_index ^ 3)), "seq", near)
-    for_far = product(part(seq_index ^ 2))
-    from_far = lax.ppermute((widened(for_far) + widened(from_near)).astype(jnp.bfloat16), "seq", far)
-    own_near = lax.ppermute(product(part(seq_index ^ 1)), "seq", near)
-    own = product(part(seq_index))
-    return (widened(own) + widened(own_near) + widened(from_far)).astype(jnp.bfloat16)
+    def one(pair, which):
+        return lax.dynamic_index_in_dim(pair, which, 0, keepdims=False)
+
+    away, home = halves(1 - half), halves(half)
+    far_context = lax.ppermute(away, "seq", far)
+    from_near = lax.ppermute(
+        product(one(away, 1 - core), tail_weight).astype(jnp.bfloat16), "seq", near
+    )
+    for_far = product(one(away, core), tail_weight) + from_near.astype(jnp.float32)
+    from_far = lax.ppermute(for_far.astype(jnp.bfloat16), "seq", far)
+
+    def head_sum(which):
+        return product(one(home, which), head_weight) + product(
+            one(far_context, which), far_weight
+        )
+
+    near_tail = lax.ppermute(
+        product(one(home, 1 - core), tail_weight).astype(jnp.bfloat16), "seq", near
+    )
+    near_head = lax.ppermute(head_sum(1 - core).astype(jnp.bfloat16), "seq", near)
+    own_tail = product(one(home, core), tail_weight)
+    head = head_sum(core) + near_head.astype(jnp.float32)
+    tail = own_tail + near_tail.astype(jnp.float32) + from_far.astype(jnp.float32)
+    return jnp.concatenate([head.astype(jnp.bfloat16), tail.astype(jnp.bfloat16)], axis=1)
 
 
 def per_device(tokens, positions, loss_mask, sample_tokens, dest_slot, norm_gain, q_weight, k_weight,
@@ -193,16 +230,16 @@
     kv_count = k_cols // DH
     group_size = q_cols // k_cols
     cols = q_cols + k_cols + v_cols
+    far_weight = None
+    if seq_count == 4:
+        far_weight = lax.ppermute(
+            o_weight[:, : early_columns(o_weight.shape[1])], "seq", partners(seq_count, 2)
+        )
     peer = dest_slot // slots
     code = dest_slot % slots + 1
-    lane = jnp.arange(META, dtype=jnp.int32)[None, :]
-    meta = jnp.where(
-        lane == 0,
-        (code // RADIX)[:, None],
-        jnp.where(lane == 1, (code % RADIX)[:, None], jnp.where(lane < 5, loss_mask[:, None], 0)),
-    ).astype(jnp.bfloat16)
-    cosine, sine = rotary_tables(positions, DH)
-    bias = jnp.concatenate([q_bias, k_bias, v_bias])[None, :]
+    digits = [d for p in (positions[0], positions[1], positions[2], code)
+              for d in (p // RADIX, p % RADIX)]
+    info = jnp.stack(digits + [loss_mask, peer] + [jnp.zeros_like(peer)] * 6).astype(jnp.bfloat16)
     chunk = chunk_of(width, 512)
     whole = lambda *shape: pl.BlockSpec(shape, lambda i: (0, 0))
     down = lambda n: pl.BlockSpec((chunk, n), lambda i: (i, 0))
@@ -211,15 +248,16 @@
         lambda *refs: send_kernel(capacity, width, *refs),
         name="project_and_pack",
         grid=(width // chunk,),
-        in_specs=[across(rows), across(1), down(q_cols), down(k_cols), down(v_cols), whole(1, cols),
-                  whole(rows, DH), whole(rows, DH), whole(1, rows), whole(rows, 1),
-                  whole(rows, META)],
+        in_specs=[across(rows), whole(width // 128, 128), down(q_cols), down(k_cols), down(v_cols),
+                  whole(q_cols // DH, DH), whole(k_cols // DH, DH), whole(v_cols // DH, DH),
+                  whole(*info.shape)],
         out_specs=whole(slots, cols + META),
         out_shape=jax.ShapeDtypeStruct((slots, cols + META), jnp.bfloat16),
         scratch_shapes=[pltpu.VMEM((rows, cols), jnp.float32), pltpu.VMEM((rows, 128), jnp.float32),
-                        pltpu.VMEM((slots, rows), jnp.bfloat16)],
-    )(tokens, norm_gain[None, :], q_weight, k_weight, v_weight, bias, cosine, sine, peer[None, :],
-      peer[:, None], meta)
+                        pltpu.VMEM((slots, rows), jnp.bfloat16), pltpu.VMEM((rows, DH), jnp.float32),
+                        pltpu.VMEM((rows, DH), jnp.float32), pltpu.VMEM((rows, META), jnp.bfloat16)],
+    )(tokens, norm_gain.reshape(-1, 128), q_weight, k_weight, v_weight, q_bias.reshape(-1, DH),
+      k_bias.reshape(-1, DH), v_bias.reshape(-1, DH), info)
     recv = lax.all_to_all(
         send.reshape(peer_count, capacity, cols + META), "dp", split_axis=0, concat_axis=0, tiled=True
     ).reshape(slots, cols + META)
@@ -235,7 +273,7 @@
     )(lengths, recv)
     part_rows = slots // seq_count
     own_weights = lax.dynamic_slice_in_dim(weights[0], seq_index * part_rows, part_rows, 0)
-    return sum_groups(context, o_weight, seq_count, seq_index), own_weights
+    return sum_groups(context, o_weight, far_weight, seq_count, seq_index), own_weights
 
 
 def solution(mesh):

time: 119 us -> 112 us (0.941)
  matrix products: 13.5 us -> 7.58 us
  other arithmetic: 8.48 us -> 5.12 us
  starting transfers between devices: 9.4 us -> 12.7 us
  waiting for transfers between devices: 58.7 us -> 56.9 us
    dot_general x4 -> x8, matrix products: 13.5 us -> 7.58 us  [product(): return jnp.dot(rows, weight, preferred_element_type=jnp.float32)]
    all_to_all x1, waiting for transfers between devices: 32.1 us -> 27.2 us  [per_device(): lax.all_to_all(send.reshape(peer_count, capacity, cols + META), 'dp', spl...]
    convert_element_type x2 -> x1, other arithmetic: 4.58 us -> 0.16 us  [sum_groups(): tail.astype(jnp.bfloat16)]
    another operation x0 -> x5, other arithmetic: none -> 3.79 us
    broadcast_in_dim x4 -> x0, local copies, waits for them, and re-layouts: 3.36 us -> none  [the longest x1 1.34 us: per_device(): norm_gain[None, :]]
    ppermute x3 -> x6, starting transfers between devices: 2.1 us -> 5.37 us  [the longest x1 1.62 us: sum_groups(): from_far = lax.ppermute(for_far.astype(jnp.bfloat16), 'seq', far)]
    ppermute x3 -> x6, waiting for transfers between devices: 26.6 us -> 29.6 us  [the longest x1 14.6 us: per_device(): lax.ppermute(o_weight[:, :early_columns(o_weight.shape[1])], 'seq', partn...]
    slice x1, local copies, waits for them, and re-layouts: 0.84 us -> 3.42 us  [sum_groups(): head_weight, tail_weight = (o_weight[:, :early], o_weight[:, early:])]
  transfers between devices with their start and end apart: 4 -> 7, of which waited for: 2 -> 4; matrix products, arithmetic and copies ran while one was open for 10% -> 12% of each run, Pallas kernels for 0% -> 7%
where the time goes in v2:
time: 112 us; the launch traced here: 111 us
  waiting for transfers between devices  56.9 us (51%)
  Pallas kernels  20.4 us (18%)
  starting transfers between devices  12.7 us (11%)
  local copies, waits for them, and re-layouts  8.02 us (7%)
  matrix products  7.58 us (7%)
  other arithmetic  5.12 us (5%)
    all_to_all x1, waiting for transfers between devices, per_device(): lax.all_to_all(send.reshape(peer_count, capacity, cols + META), 'dp', spl...  27.2 us
    ppermute x1, waiting for transfers between devices, per_device(): lax.ppermute(o_weight[:, :early_columns(o_weight.shape[1])], 'seq', partn...  14.6 us
    pallas_call x1, Pallas kernels, per_device(): pl.pallas_call(lambda *refs: send_kernel(capacity, width, *refs), name='p...  13.1 us
    ppermute x1, waiting for transfers between devices, sum_groups(): from_far = lax.ppermute(for_far.astype(jnp.bfloat16), 'seq', far)  7.99 us
    dot_general x8, matrix products, product(): return jnp.dot(rows, weight, preferred_element_type=jnp.float32)  7.58 us
    all_to_all x1, starting transfers between devices, per_device(): lax.all_to_all(send.reshape(peer_count, capacity, cols + META), 'dp', spl...  7.31 us
    pallas_call x1, Pallas kernels, per_device(): pl.pallas_call(lambda *refs: attend_kernel(float(peer_count * rows), kv_c...  7.28 us
    ppermute x1, waiting for transfers between devices, sum_groups(): far_context = lax.ppermute(away, 'seq', far)  6.98 us
  transfers between devices with their start and end apart: 7, of which 4 were waited for; matrix products, arithmetic and copies ran while one was open for 12% of the time, Pallas kernels for 7%

profile of v2, /device:TPU:0, one launch (start us, length us, event | category | flops | bytes accessed | tf_op | source)
XLA Modules:
  0.0 111.4 jit_solution(2369661833792282023)
XLA Ops:
  0.6 0.0 copy-start
  0.6 0.8 fusion.38
  1.5 0.9 fusion.36
  2.3 0.7 fusion.39
  3.0 0.7 fusion.32
  3.8 0.7 convert.46
  4.5 1.3 %stack.38.refs_8_ = bf16[16,576]{1,0:T(8,128)(2,1)} concatenate(bf16[1,576]{1,0:T(2,128)(2,1)S(1)} %fusion.39, bf16[1,576]{1,0:T(2,128)(2,1)S(1)} %get-tuple-element.10, bf16[1,576]{1,0:T(2,128)(2,1)S(1)} %get-tuple-element.15, bf16[1,576]{1,0:T(2,128)(2,1)S(1)} %get-tuple-element.13, bf16[1,576]{1,0:T(2,128)(2,1)S(1)} %get-tuple-element.12, ...), dimensions={0} | concatenate | bytes 36864 | tf_op jit(solution)/shard_map/stack | solution.py:242
  5.8 13.1 %project_and_pack.1 = bf16[768,896]{1,0:T(8,128)(2,1)} custom-call(bf16[576,3584]{1,0:T(8,128)(2,1)} %refs_0_.1, f32[28,128]{1,0:T(8,128)} %bitcast.42, bf16[3584,512]{1,0:T(8,128)(2,1)} %refs_2_.1, bf16[3584,128]{1,0:T(8,128)(2,1)} %refs_3_.1, bf16[3584,128]{1,0:T(8,128)(2,1)} %refs_4_.1, f32[4,128]{1,0:T(4,128)} %bitcast.43, f32[1,128]{1,0:T(1,128)} %bitcast.45, ...), custom_call_target="tpu_custom_call" | custom-call | tf_op jit(solution)/shard_map/project_and_pack/pallas_call | solution.py:247
  18.8 7.3 %all-to-all-start = ((bf16[8,96,896]{2,1,0:T(8,128)(2,1)}), bf16[8,96,896]{2,1,0:T(8,128)(2,1)}, u32[]{:S(2)}, u32[]{:S(2)}) async-start(bf16[8,96,896]{2,1,0:T(8,128)(2,1)} %bitcast.34), calls=%async_computation | async-start | bytes 2752512 | tf_op jit(solution)/shard_map/all_to_all | solution.py:261
  26.2 3.4 %slice.19 = bf16[512,2560]{1,0:T(8,128)(2,1)} slice(bf16[512,3584]{1,0:T(8,128)(2,1)} %param.25), slice={[0:512], [0:2560]} | slice | bytes 5242880 | tf_op jit(solution)/shard_map/slice | solution.py:187
  29.6 1.5 %collective-permute-start.1 = (bf16[512,2560]{1,0:T(8,128)(2,1)}, bf16[512,2560]{1,0:T(8,128)(2,1)S(1)}, u32[]{:S(2)}, u32[]{:S(2)}) collective-permute-start(bf16[512,2560]{1,0:T(8,128)(2,1)} %slice.19), channel_id=1, source_target_pairs={{0,2},{1,3},{2,0},{3,1},{4,6},{5,7},{6,4},{7,5},{8,10},{9,11},{10,... | collective-permute-start | bytes 7864328 | tf_op jit(solution)/shard_map/ppermute | solution.py:235
  31.1 0.0 copy-done
  31.1 0.7 fusion.50.refs_0_
  31.8 27.2 %all-to-all-done = bf16[8,96,896]{2,1,0:T(8,128)(2,1)} async-done(((bf16[8,96,896]{2,1,0:T(8,128)(2,1)}), bf16[8,96,896]{2,1,0:T(8,128)(2,1)}, u32[]{:S(2)}, u32[]{:S(2)}) %all-to-all-start) | async-done | bytes 1376288 | tf_op jit(solution)/shard_map/all_to_all | solution.py:261
  59.0 7.3 %place_and_attend.1 = (bf16[768,512]{1,0:T(8,128)(2,1)}, f32[1,768]{1,0:T(1,128)}) custom-call(s32[3]{0:T(128)} %fusion.50.refs_0_, bf16[768,896]{1,0:T(8,128)(2,1)} %bitcast.5.refs_1_), custom_call_target="tpu_custom_call" | custom-call | tf_op jit(solution)/shard_map/place_and_attend/pallas_call | solution.py:265
  66.3 0.0 copy-start.2
  66.3 1.1 dynamic-slice_bitcast_fusion
  67.4 1.6 %collective-permute-start = (bf16[2,192,512]{2,1,0:T(8,128)(2,1)S(1)}, bf16[2,192,512]{2,1,0:T(8,128)(2,1)S(1)}, u32[]{:S(2)}, u32[]{:S(2)}) collective-permute-start(bf16[2,192,512]{2,1,0:T(8,128)(2,1)S(1)} %dynamic-slice_bitcast_fusion), channel_id=1, source_target_pairs={{0,2},{1,3},{2,0},{3,1},{4,6},{5,7},{6,4},{7,5},{8,10},{9,11},{10,... | collective-permute-start | bytes 1179656 | tf_op jit(solution)/shard_map/ppermute | solution.py:198
  69.0 1.7 %convolution_convert_fusion.1 = bf16[192,1024]{1,0:T(8,128)(2,1)S(1)} fusion(bf16[512,3584]{1,0:T(8,128)(2,1)} %param.25, bf16[2,2,192,512]{3,2,1,0:T(8,128)(2,1)} %bitcast.36, s32[]{:T(128)S(6)} %select_n.103, s32[]{:T(128)S(6)} %select_n.109), kind=kOutput, calls=%fused_computation.7 | convolution fusion | flops 201523200 | bytes 1638408 | tf_op jit(solution)/shard_map/dot_general | solution.py:178
  70.7 0.0 copy-done.2
  70.7 0.0 copy-start.1
  70.7 2.6 %fusion.15 = f32[192,2560]{1,0:T(8,128)S(1)} fusion(bf16[2,2,192,512]{3,2,1,0:T(8,128)(2,1)S(1)} %bitcast.37, s32[]{:T(128)S(6)} %select_n.103, s32[]{:T(128)S(6)} %select_n.109, bf16[512,3584]{1,0:T(8,128)(2,1)} %param.25), kind=kOutput, calls=%fused_computation.21 | convolution fusion | flops 503316480 | bytes 4784136 | tf_op jit(solution)/shard_map/dot_general | solution.py:178
  73.3 0.2 copy-done.1
  73.6 0.4 convolution_convert_fusion
  73.9 0.1 collective-permute-start.4
  74.0 0.5 collective-permute-start.3
  74.5 0.4 fusion.7
  74.9 14.6 %collective-permute-done.1 = bf16[512,2560]{1,0:T(8,128)(2,1)S(1)} collective-permute-done((bf16[512,2560]{1,0:T(8,128)(2,1)}, bf16[512,2560]{1,0:T(8,128)(2,1)S(1)}, u32[]{:S(2)}, u32[]{:S(2)}) %collective-permute-start.1) | collective-permute-done | bytes 2621472 | tf_op jit(solution)/shard_map/ppermute | solution.py:235
  89.5 7.0 %collective-permute-done = bf16[2,192,512]{2,1,0:T(8,128)(2,1)S(1)} collective-permute-done((bf16[2,192,512]{2,1,0:T(8,128)(2,1)S(1)}, bf16[2,192,512]{2,1,0:T(8,128)(2,1)S(1)}, u32[]{:S(2)}, u32[]{:S(2)}) %collective-permute-start) | collective-permute-done | bytes 393248 | tf_op jit(solution)/shard_map/ppermute | solution.py:198
  96.5 0.7 fusion.1
  97.2 0.1 collective-permute-start.2
  97.3 0.0 collective-permute-done.4
  97.3 0.4 add_convert_fusion.1
  97.7 1.6 %collective-permute-start.5 = (bf16[192,1024]{1,0:T(8,128)(2,1)S(1)}, bf16[192,1024]{1,0:T(8,128)(2,1)S(1)}, u32[]{:S(2)}, u32[]{:S(2)}) collective-permute-start(bf16[192,1024]{1,0:T(8,128)(2,1)S(1)} %add_convert_fusion.1), channel_id=1, source_target_pairs={{0,2},{1,3},{2,0},{3,1},{4,6},{5,7},{6,4},{7,5},{8,10},{9,11},{10,... | collective-permute-start | bytes 1179656 | tf_op jit(solution)/shard_map/ppermute | solution.py:203
  99.3 1.3 %constant_dynamic-slice_fusion = f32[1,192]{1,0:T(1,128)} fusion(f32[1,768]{1,0:T(1,128)} %get-tuple-element.5, s32[]{:T(128)S(6)} %select_n.111), kind=kLoop, calls=%fused_computation.75 | loop fusion | bytes 1540 | tf_op jit(solution)/shard_map/dynamic_slice | solution.py:275
  100.6 0.7 fusion.19
  101.3 0.0 collective-permute-done.3
  101.3 8.0 %collective-permute-done.5 = bf16[192,1024]{1,0:T(8,128)(2,1)S(1)} collective-permute-done((bf16[192,1024]{1,0:T(8,128)(2,1)S(1)}, bf16[192,1024]{1,0:T(8,128)(2,1)S(1)}, u32[]{:S(2)}, u32[]{:S(2)}) %collective-permute-start.5) | collective-permute-done | bytes 393248 | tf_op jit(solution)/shard_map/ppermute | solution.py:203
  109.3 0.2 add_convert_fusion
  109.5 0.0 collective-permute-done.2
  109.5 0.8 fusion.2
  110.2 1.2 %pad_maximum_fusion = bf16[192,3584]{1,0:T(8,128)(2,1)} fusion(bf16[192,1024]{1,0:T(8,128)(2,1)S(1)} %add_convert_fusion, bf16[192,2560]{1,0:T(8,128)(2,1)S(1)} %fusion.2), kind=kLoop, calls=%fused_computation.5 | loop fusion | flops 2752512 | bytes 2752512 | tf_op jit(solution)/shard_map/concatenate | solution.py:217
  (6 shorter events, 0.0 us)
Async XLA Ops:
  0.6 30.5 %copy-start = (s32[8,3]{0,1:T(4,128)S(1)}, s32[8,3]{0,1:T(4,128)}, u32[]{:S(2)}) copy-start(s32[8,3]{0,1:T(4,128)} %param.16) | copy-start | bytes 292
  18.8 40.2 %all-to-all-start = ((bf16[8,96,896]{2,1,0:T(8,128)(2,1)}), bf16[8,96,896]{2,1,0:T(8,128)(2,1)}, u32[]{:S(2)}, u32[]{:S(2)}) async-start(bf16[8,96,896]{2,1,0:T(8,128)(2,1)} %bitcast.34), calls=%async_computation | async-start | bytes 2752512 | tf_op jit(solution)/shard_map/all_to_all | solution.py:261
  29.6 59.9 %collective-permute-start.1 = (bf16[512,2560]{1,0:T(8,128)(2,1)}, bf16[512,2560]{1,0:T(8,128)(2,1)S(1)}, u32[]{:S(2)}, u32[]{:S(2)}) collective-permute-start(bf16[512,2560]{1,0:T(8,128)(2,1)} %slice.19), channel_id=1, source_target_pairs={{0,2},{1,3},{2,0},{3,1},{4,6},{5,7},{6,4},{7,5},{8,10},{9,11},{10,... | collective-permute-start | bytes 7864328 | tf_op jit(solution)/shard_map/ppermute | solution.py:235
  66.3 4.4 %copy-start.2 = (bf16[768,512]{1,0:T(8,128)(2,1)S(1)}, bf16[768,512]{1,0:T(8,128)(2,1)}, u32[]{:S(2)}) copy-start(bf16[768,512]{1,0:T(8,128)(2,1)} %get-tuple-element.4) | copy-start | bytes 2359300
  67.4 29.1 %collective-permute-start = (bf16[2,192,512]{2,1,0:T(8,128)(2,1)S(1)}, bf16[2,192,512]{2,1,0:T(8,128)(2,1)S(1)}, u32[]{:S(2)}, u32[]{:S(2)}) collective-permute-start(bf16[2,192,512]{2,1,0:T(8,128)(2,1)S(1)} %dynamic-slice_bitcast_fusion), channel_id=1, source_target_pairs={{0,2},{1,3},{2,0},{3,1},{4,6},{5,7},{6,4},{7,5},{8,10},{9,11},{10,... | collective-permute-start | bytes 1179656 | tf_op jit(solution)/shard_map/ppermute | solution.py:198
  70.7 2.8 %copy-start.1 = (bf16[512,3584]{1,0:T(8,128)(2,1)S(1)}, bf16[512,3584]{1,0:T(8,128)(2,1)}, u32[]{:S(2)}) copy-start(bf16[512,3584]{1,0:T(8,128)(2,1)} %param.25) | copy-start | bytes 11010052
  73.9 23.4 %collective-permute-start.4 = (bf16[192,1024]{1,0:T(8,128)(2,1)S(1)}, bf16[192,1024]{1,0:T(8,128)(2,1)S(1)}, u32[]{:S(2)}, u32[]{:S(2)}) collective-permute-start(bf16[192,1024]{1,0:T(8,128)(2,1)S(1)} %convolution_convert_fusion), channel_id=1, source_target_pairs={{0,1},{1,0},{2,3},{3,2},{4,5},{5,4},{6,7},{7,6},{8,9},{9,8},{10,11... | collective-permute-start | bytes 1179656 | tf_op jit(solution)/shard_map/ppermute | solution.py:199
  74.0 27.3 %collective-permute-start.3 = (bf16[192,1024]{1,0:T(8,128)(2,1)S(1)}, bf16[192,1024]{1,0:T(8,128)(2,1)S(1)}, u32[]{:S(2)}, u32[]{:S(2)}) collective-permute-start(bf16[192,1024]{1,0:T(8,128)(2,1)S(1)} %convolution_convert_fusion.1), channel_id=1, source_target_pairs={{0,1},{1,0},{2,3},{3,2},{4,5},{5,4},{6,7},{7,6},{8,9},{9,8},{10,11... | collective-permute-start | bytes 1179656 | tf_op jit(solution)/shard_map/ppermute | solution.py:210
  97.2 12.2 %collective-permute-start.2 = (bf16[192,2560]{1,0:T(8,128)(2,1)S(1)}, bf16[192,2560]{1,0:T(8,128)(2,1)S(1)}, u32[]{:S(2)}, u32[]{:S(2)}) collective-permute-start(bf16[192,2560]{1,0:T(8,128)(2,1)S(1)} %fusion.1), channel_id=1, source_target_pairs={{0,1},{1,0},{2,3},{3,2},{4,5},{5,4},{6,7},{7,6},{8,9},{9,8},{10,11... | collective-permute-start | bytes 2949128 | tf_op jit(solution)/shard_map/ppermute | solution.py:213
  97.7 11.6 %collective-permute-start.5 = (bf16[192,1024]{1,0:T(8,128)(2,1)S(1)}, bf16[192,1024]{1,0:T(8,128)(2,1)S(1)}, u32[]{:S(2)}, u32[]{:S(2)}) collective-permute-start(bf16[192,1024]{1,0:T(8,128)(2,1)S(1)} %add_convert_fusion.1), channel_id=1, source_target_pairs={{0,2},{1,3},{2,0},{3,1},{4,6},{5,7},{6,4},{7,5},{8,10},{9,11},{10,... | collective-permute-start | bytes 1179656 | tf_op jit(solution)/shard_map/ppermute | solution.py:203

commit v3 on v2

--- a/solution.py
+++ b/solution.py
@@ -33,7 +33,8 @@
 
 
 def send_kernel(capacity, width, x_ref, gain_ref, wq_ref, wk_ref, wv_ref, bq_ref, bk_ref, bv_ref,
-                info_ref, out_ref, acc_ref, sq_ref, sel_ref, cos_ref, sin_ref, meta_ref):
+                pos_ref, mask_ref, dest_ref, out_ref, acc_ref, sq_ref, sel_ref, cos_ref, sin_ref,
+                meta_ref, info_ref):
     step = pl.program_id(0)
     rows, chunk = x_ref.shape
     q_cols, k_cols = wq_ref.shape[1], wk_ref.shape[1]
@@ -43,7 +44,18 @@
     def _():
         acc_ref[...] = jnp.zeros_like(acc_ref)
         sq_ref[...] = jnp.zeros_like(sq_ref)
-        info = info_ref[...]
+        dest = dest_ref[...].astype(jnp.float32)
+        peer_row = jnp.floor((dest + 0.5) * (1.0 / slots))
+        code = dest - peer_row * slots + 1.0
+        info_ref[...] = jnp.zeros_like(info_ref)
+        numbers = [pos_ref[i : i + 1].astype(jnp.float32) for i in range(3)] + [code]
+        for i, number in enumerate(numbers):
+            high = jnp.floor(number * (1.0 / RADIX))
+            info_ref[2 * i : 2 * i + 1] = high
+            info_ref[2 * i + 1 : 2 * i + 2] = number - RADIX * high
+        info_ref[8:9] = mask_ref[...].astype(jnp.float32)
+        info_ref[9:10] = peer_row
+        info = info_ref[...].astype(jnp.bfloat16)
 
         def columns(weights):
             return lax.dot_general(info, weights.astype(jnp.bfloat16), (((0,), (0,)), ((), ())),
@@ -56,7 +68,6 @@
         angles = ids * jnp.exp(pair * (-2.0 * math.log(ROPE_BASE) / DH))
         cos_ref[...] = jnp.cos(angles)
         sin_ref[...] = jnp.sin(angles) * jnp.where(lane < DH // 2, -1.0, 1.0)
-        peer_row = info[9:10].astype(jnp.float32)
         first = lax.broadcasted_iota(jnp.int32, (rows, rows), 0)
         second = lax.broadcasted_iota(jnp.int32, (rows, rows), 1)
         before = (peers[:, :1] == peer_row) & (first < second)
@@ -167,7 +178,8 @@
 
 
 def early_columns(width):
-    return width * 5 // 7 // 128 * 128
+    first = width // 7 // 128 * 128
+    return first, 4 * first
 
 
 def partners(seq_count, bit):
@@ -178,13 +190,15 @@
     return jnp.dot(rows, weight, preferred_element_type=jnp.float32)
 
 
-def sum_groups(context, o_weight, far_weight, seq_count, seq_index):
+def sum_groups(context, o_weight, far_weights, seq_count, seq_index):
     if seq_count != 4:
         partial = product(context, o_weight).astype(jnp.bfloat16)
         return lax.psum_scatter(partial, "seq", scatter_dimension=0, tiled=True)
     near, far = partners(seq_count, 1), partners(seq_count, 2)
-    early = far_weight.shape[1]
-    head_weight, tail_weight = o_weight[:, :early], o_weight[:, early:]
+    cuts = [0]
+    for weight in far_weights:
+        cuts.append(cuts[-1] + weight.shape[1])
+    tail_weight = o_weight[:, cuts[-1] :]
     parts = context.reshape(2, 2, -1, context.shape[1])
     half, core = seq_index // 2, seq_index % 2
 
@@ -203,18 +217,21 @@
     from_far = lax.ppermute(for_far.astype(jnp.bfloat16), "seq", far)
 
     def head_sum(which):
-        return product(one(home, which), head_weight) + product(
-            one(far_context, which), far_weight
-        )
+        return [
+            product(one(home, which), o_weight[:, low:high]) + product(one(far_context, which), weight)
+            for low, high, weight in zip(cuts, cuts[1:], far_weights)
+        ]
 
     near_tail = lax.ppermute(
         product(one(home, 1 - core), tail_weight).astype(jnp.bfloat16), "seq", near
     )
-    near_head = lax.ppermute(head_sum(1 - core).astype(jnp.bfloat16), "seq", near)
+    near_heads = [
+        lax.ppermute(head.astype(jnp.bfloat16), "seq", near) for head in head_sum(1 - core)
+    ]
     own_tail = product(one(home, core), tail_weight)
-    head = head_sum(core) + near_head.astype(jnp.float32)
+    heads = [head + got.astype(jnp.float32) for head, got in zip(head_sum(core), near_heads)]
     tail = own_tail + near_tail.astype(jnp.float32) + from_far.astype(jnp.float32)
-    return jnp.concatenate([head.astype(jnp.bfloat16), tail.astype(jnp.bfloat16)], axis=1)
+    return jnp.concatenate([piece.astype(jnp.bfloat16) for piece in heads + [tail]], axis=1)
 
 
 def per_device(tokens, positions, loss_mask, sample_tokens, dest_slot, norm_gain, q_weight, k_weight,
@@ -230,16 +247,6 @@
     kv_count = k_cols // DH
     group_size = q_cols // k_cols
     cols = q_cols + k_cols + v_cols
-    far_weight = None
-    if seq_count == 4:
-        far_weight = lax.ppermute(
-            o_weight[:, : early_columns(o_weight.shape[1])], "seq", partners(seq_count, 2)
-        )
-    peer = dest_slot // slots
-    code = dest_slot % slots + 1
-    digits = [d for p in (positions[0], positions[1], positions[2], code)
-              for d in (p // RADIX, p % RADIX)]
-    info = jnp.stack(digits + [loss_mask, peer] + [jnp.zeros_like(peer)] * 6).astype(jnp.bfloat16)
     chunk = chunk_of(width, 512)
     whole = lambda *shape: pl.BlockSpec(shape, lambda i: (0, 0))
     down = lambda n: pl.BlockSpec((chunk, n), lambda i: (i, 0))
@@ -250,14 +257,23 @@
         grid=(width // chunk,),
         in_specs=[across(rows), whole(width // 128, 128), down(q_cols), down(k_cols), down(v_cols),
                   whole(q_cols // DH, DH), whole(k_cols // DH, DH), whole(v_cols // DH, DH),
-                  whole(*info.shape)],
+                  whole(3, rows), whole(1, rows), whole(1, rows)],
         out_specs=whole(slots, cols + META),
         out_shape=jax.ShapeDtypeStruct((slots, cols + META), jnp.bfloat16),
         scratch_shapes=[pltpu.VMEM((rows, cols), jnp.float32), pltpu.VMEM((rows, 128), jnp.float32),
                         pltpu.VMEM((slots, rows), jnp.bfloat16), pltpu.VMEM((rows, DH), jnp.float32),
-                        pltpu.VMEM((rows, DH), jnp.float32), pltpu.VMEM((rows, META), jnp.bfloat16)],
+                        pltpu.VMEM((rows, DH), jnp.float32), pltpu.VMEM((rows, META), jnp.bfloat16),
+                        pltpu.VMEM((16, rows), jnp.float32)],
     )(tokens, norm_gain.reshape(-1, 128), q_weight, k_weight, v_weight, q_bias.reshape(-1, DH),
-      k_bias.reshape(-1, DH), v_bias.reshape(-1, DH), info)
+      k_bias.reshape(-1, DH), v_bias.reshape(-1, DH), positions,
+      loss_mask[None, :], dest_slot[None, :])
+    far_weights = ()
+    if seq_count == 4:
+        first, early = early_columns(o_weight.shape[1])
+        far = partners(seq_count, 2)
+        far_first = lax.ppermute(o_weight[:, :first], "seq", far)
+        send, far_first, later = lax.optimization_barrier((send, far_first, o_weight))
+        far_weights = (far_first, lax.ppermute(later[:, first:early], "seq", far))
     recv = lax.all_to_all(
         send.reshape(peer_count, capacity, cols + META), "dp", split_axis=0, concat_axis=0, tiled=True
     ).reshape(slots, cols + META)
@@ -273,7 +289,7 @@
     )(lengths, recv)
     part_rows = slots // seq_count
     own_weights = lax.dynamic_slice_in_dim(weights[0], seq_index * part_rows, part_rows, 0)
-    return sum_groups(context, o_weight, far_weight, seq_count, seq_index), own_weights
+    return sum_groups(context, o_weight, far_weights, seq_count, seq_index), own_weights
 
 
 def solution(mesh):

time: 112 us -> 97.1 us (0.87)
  waiting for transfers between devices: 56.9 us -> 44.1 us
  other arithmetic: 5.12 us -> 1.36 us
  local copies, waits for them, and re-layouts: 8.02 us -> 10.6 us
    ppermute x2 -> x4, waiting for transfers between devices: 14.6 us -> 0.01 us  [the longest x2 0.01 us: sum_groups(): lax.ppermute(head.astype(jnp.bfloat16), 'seq', near)]
    ppermute x1, waiting for transfers between devices: 7.99 us -> 12.6 us  [sum_groups(): from_far = lax.ppermute(for_far.astype(jnp.bfloat16), 'seq', far)]
    ppermute x1, waiting for transfers between devices: 6.98 us -> 2.84 us  [sum_groups(): far_context = lax.ppermute(away, 'seq', far)]
    another operation x5 -> x0, other arithmetic: 3.79 us -> none
    ppermute x2 -> x4, starting transfers between devices: 1.57 us -> 4.18 us  [the longest x1 3.06 us: per_device(): far_first = lax.ppermute(o_weight[:, :first], 'seq', far)]
    broadcast_in_dim x0 -> x2, local copies, waits for them, and re-layouts: none -> 2.55 us  [the longest x1 1.27 us: per_device(): loss_mask[None, :]]
    all_to_all x1, starting transfers between devices: 7.31 us -> 5.82 us  [per_device(): lax.all_to_all(send.reshape(peer_count, capacity, cols + META), 'dp', spl...]
    all_to_all x1, waiting for transfers between devices: 27.2 us -> 28.6 us  [per_device(): lax.all_to_all(send.reshape(peer_count, capacity, cols + META), 'dp', spl...]
  transfers between devices with their start and end apart: 7 -> 9, of which waited for: 4 -> 3; matrix products, arithmetic and copies ran while one was open for 12% -> 16% of each run, Pallas kernels for 7% -> 21%
where the time goes in v3:
time: 97.1 us; the launch traced here: 96.6 us
  waiting for transfers between devices  44.1 us (45%)
  Pallas kernels  20.5 us (21%)
  starting transfers between devices  11.8 us (12%)
  local copies, waits for them, and re-layouts  10.6 us (11%)
  matrix products  7.44 us (8%)
  other arithmetic  1.36 us (1%)
    all_to_all x1, waiting for transfers between devices, per_device(): lax.all_to_all(send.reshape(peer_count, capacity, cols + META), 'dp', spl...  28.6 us
    pallas_call x1, Pallas kernels, per_device(): pl.pallas_call(lambda *refs: send_kernel(capacity, width, *refs), name='p...  13.3 us
    ppermute x1, waiting for transfers between devices, sum_groups(): from_far = lax.ppermute(for_far.astype(jnp.bfloat16), 'seq', far)  12.6 us
    dot_general x12, matrix products, product(): return jnp.dot(rows, weight, preferred_element_type=jnp.float32)  7.44 us
    pallas_call x1, Pallas kernels, per_device(): pl.pallas_call(lambda *refs: attend_kernel(float(peer_count * rows), kv_c...  7.27 us
    all_to_all x1, starting transfers between devices, per_device(): lax.all_to_all(send.reshape(peer_count, capacity, cols + META), 'dp', spl...  5.82 us
    ppermute x1, starting transfers between devices, per_device(): far_first = lax.ppermute(o_weight[:, :first], 'seq', far)  3.06 us
    ppermute x1, waiting for transfers between devices, sum_groups(): far_context = lax.ppermute(away, 'seq', far)  2.84 us
  transfers between devices with their start and end apart: 9, of which 3 were waited for; matrix products, arithmetic and copies ran while one was open for 16% of the time, Pallas kernels for 21%

profile of v3, /device:TPU:0, one launch (start us, length us, event | category | flops | bytes accessed | tf_op | source)
XLA Modules:
  0.0 96.6 jit_solution(14145707650956756624)
XLA Ops:
  0.6 0.0 copy-start
  0.6 1.1 %slice.15 = bf16[512,512]{1,0:T(8,128)(2,1)S(1)} slice(bf16[512,3584]{1,0:T(8,128)(2,1)} %param.25), slice={[0:512], [0:512]} | slice | bytes 1048576 | tf_op jit(solution)/shard_map/slice | solution.py:274
  1.7 3.1 %collective-permute-start = (bf16[512,512]{1,0:T(8,128)(2,1)S(1)}, bf16[512,512]{1,0:T(8,128)(2,1)S(1)}, u32[]{:S(2)}, u32[]{:S(2)}) collective-permute-start(bf16[512,512]{1,0:T(8,128)(2,1)S(1)} %slice.15), channel_id=1, source_target_pairs={{0,2},{1,3},{2,0},{3,1},{4,6},{5,7},{6,4},{7,5},{8,10},{9,11},{10,... | collective-permute-start | bytes 1572872 | tf_op jit(solution)/shard_map/ppermute | solution.py:274
  4.8 1.3 %broadcast_in_dim.6.refs_9_ = s32[1,576]{1,0:T(1,128)} reshape(s32[576]{0:T(1024)} %param.15) | data formatting | bytes 4608 | tf_op jit(solution)/shard_map/broadcast_in_dim | solution.py:269
  6.1 1.3 %broadcast_in_dim.7.refs_10_ = s32[1,576]{1,0:T(1,128)} reshape(s32[576]{0:T(1024)} %param.17) | data formatting | bytes 4608 | tf_op jit(solution)/shard_map/broadcast_in_dim | solution.py:269
  7.3 13.3 %project_and_pack.1 = bf16[768,896]{1,0:T(8,128)(2,1)} custom-call(bf16[576,3584]{1,0:T(8,128)(2,1)} %refs_0_.1, f32[28,128]{1,0:T(8,128)} %bitcast.55, bf16[3584,512]{1,0:T(8,128)(2,1)} %refs_2_.1, bf16[3584,128]{1,0:T(8,128)(2,1)} %refs_3_.1, bf16[3584,128]{1,0:T(8,128)(2,1)} %refs_4_.1, f32[4,128]{1,0:T(4,128)} %bitcast.56, f32[1,128]{1,0:T(1,128)} %bitcast.58, ...), custom_call_target="tpu_custom_call" | custom-call | tf_op jit(solution)/shard_map/project_and_pack/pallas_call | solution.py:254
  20.6 0.0 collective-permute-done
  20.6 5.8 %all-to-all-start = ((bf16[8,96,896]{2,1,0:T(8,128)(2,1)}), bf16[8,96,896]{2,1,0:T(8,128)(2,1)S(1)}, u32[]{:S(2)}, u32[]{:S(2)}) async-start(bf16[8,96,896]{2,1,0:T(8,128)(2,1)} %bitcast.44), calls=%async_computation | async-start | bytes 2752512 | tf_op jit(solution)/shard_map/all_to_all | solution.py:277
  26.4 0.0 copy-done
  26.4 0.7 fusion.56.refs_0_
  27.1 2.7 %slice.17 = bf16[512,1536]{1,0:T(8,128)(2,1)} slice(bf16[512,3584]{1,0:T(8,128)(2,1)} %param.25), slice={[0:512], [512:2048]} | slice | bytes 3145728 | tf_op jit(solution)/shard_map/slice | solution.py:276
  29.8 0.5 collective-permute-start.3
  30.3 28.6 %all-to-all-done = bf16[8,96,896]{2,1,0:T(8,128)(2,1)S(1)} async-done(((bf16[8,96,896]{2,1,0:T(8,128)(2,1)}), bf16[8,96,896]{2,1,0:T(8,128)(2,1)S(1)}, u32[]{:S(2)}, u32[]{:S(2)}) %all-to-all-start) | async-done | bytes 1376288 | tf_op jit(solution)/shard_map/all_to_all | solution.py:277
  58.9 0.0 copy-start.2
  58.9 1.1 %copy-done.2 = bf16[8,96,896]{2,1,0:T(8,128)(2,1)} copy-done((bf16[8,96,896]{2,1,0:T(8,128)(2,1)}, bf16[8,96,896]{2,1,0:T(8,128)(2,1)S(1)}, u32[]{:S(2)}) %copy-start.2) | copy-done | bytes 1376280
  60.0 7.3 %place_and_attend.1 = (bf16[768,512]{1,0:T(8,128)(2,1)}, f32[1,768]{1,0:T(1,128)}) custom-call(s32[3]{0:T(128)} %fusion.56.refs_0_, bf16[768,896]{1,0:T(8,128)(2,1)} %bitcast.45), custom_call_target="tpu_custom_call" | custom-call | tf_op jit(solution)/shard_map/place_and_attend/pallas_call | solution.py:281
  67.3 0.0 copy-start.1
  67.3 1.2 %dynamic-slice_bitcast_fusion = bf16[2,192,512]{2,1,0:T(8,128)(2,1)S(1)} fusion(bf16[2,2,192,512]{3,2,1,0:T(8,128)(2,1)} %bitcast.46, s32[]{:T(128)S(6)} %select_n.56), kind=kLoop, calls=%fused_computation.25 | loop fusion | bytes 786436 | tf_op jit(solution)/shard_map/jit(dynamic_index_in_dim)/squeeze | solution.py:206
  68.5 0.6 collective-permute-start.1
  69.1 2.0 %fusion.3 = f32[192,1536]{1,0:T(8,128)S(1)} fusion(bf16[512,3584]{1,0:T(8,128)(2,1)} %param.25, bf16[2,2,192,512]{3,2,1,0:T(8,128)(2,1)} %bitcast.47, s32[]{:T(128)S(6)} %select_n.52, s32[]{:T(128)S(6)} %select_n.58), kind=kOutput, calls=%fused_computation.7 | convolution fusion | flops 301989888 | bytes 2949128 | tf_op jit(solution)/shard_map/dot_general | solution.py:190
  71.1 0.0 copy-done.1
  71.1 0.0 copy-start.3
  71.1 1.5 %convolution_convert_fusion = bf16[192,1536]{1,0:T(8,128)(2,1)S(1)} fusion(bf16[512,3584]{1,0:T(8,128)(2,1)S(1)} %copy-done.1, bf16[2,2,192,512]{3,2,1,0:T(8,128)(2,1)} %bitcast.48, s32[]{:T(128)S(6)} %select_n.59, s32[]{:T(128)S(6)} %select_n.58), kind=kOutput, calls=%fused_computation.5 | convolution fusion | flops 302284800 | bytes 2359304 | tf_op jit(solution)/shard_map/dot_general | solution.py:190
  72.6 0.1 collective-permute-start.6
  72.6 0.0 copy-done.3
  72.7 0.5 convolution_convert_fusion.1
  73.1 0.5 fusion.5
  73.6 0.5 fusion.14
  74.1 0.3 fusion.24
  74.4 0.3 fusion.30
  74.6 0.6 collective-permute-start.5
  75.2 2.8 %collective-permute-done.1 = bf16[2,192,512]{2,1,0:T(8,128)(2,1)S(1)} collective-permute-done((bf16[2,192,512]{2,1,0:T(8,128)(2,1)S(1)}, bf16[2,192,512]{2,1,0:T(8,128)(2,1)S(1)}, u32[]{:S(2)}, u32[]{:S(2)}) %collective-permute-start.1) | collective-permute-done | bytes 393248 | tf_op jit(solution)/shard_map/ppermute | solution.py:212
  78.0 0.3 fusion.9
  78.3 0.1 collective-permute-start.2
  78.4 0.0 collective-permute-done.3
  78.4 0.5 fusion.2
  78.9 0.6 collective-permute-start.4
  79.4 0.0 collective-permute-done.6
  79.4 0.5 add_convert_fusion.1
  79.9 0.6 collective-permute-start.7
  80.5 1.3 %constant_dynamic-slice_fusion = f32[1,192]{1,0:T(1,128)} fusion(f32[1,768]{1,0:T(1,128)} %get-tuple-element.11, s32[]{:T(128)S(6)} %select_n.60), kind=kLoop, calls=%fused_computation.58 | loop fusion | bytes 1540 | tf_op jit(solution)/shard_map/dynamic_slice | solution.py:291
  81.8 0.0 collective-permute-done.2
  81.8 0.3 fusion.8
  82.1 0.0 collective-permute-done.4
  82.1 0.5 fusion.1
  82.6 0.0 collective-permute-done.5
  82.6 12.6 %collective-permute-done.7 = bf16[192,1536]{1,0:T(8,128)(2,1)S(1)} collective-permute-done((bf16[192,1536]{1,0:T(8,128)(2,1)S(1)}, bf16[192,1536]{1,0:T(8,128)(2,1)S(1)}, u32[]{:S(2)}, u32[]{:S(2)}) %collective-permute-start.7) | collective-permute-done | bytes 589856 | tf_op jit(solution)/shard_map/ppermute | solution.py:217
  95.3 0.2 add_convert_fusion
  95.4 1.2 %pad_maximum_fusion = bf16[192,3584]{1,0:T(8,128)(2,1)} fusion(bf16[192,1536]{1,0:T(8,128)(2,1)S(1)} %add_convert_fusion, bf16[192,1536]{1,0:T(8,128)(2,1)S(1)} %fusion.1, bf16[192,512]{1,0:T(8,128)(2,1)S(1)} %fusion.8), kind=kLoop, calls=%fused_computation.11 | loop fusion | flops 4128768 | bytes 2752512 | tf_op jit(solution)/shard_map/concatenate | solution.py:234
Async XLA Ops:
  0.6 25.8 %copy-start = (s32[8,3]{0,1:T(4,128)S(1)}, s32[8,3]{0,1:T(4,128)}, u32[]{:S(2)}) copy-start(s32[8,3]{0,1:T(4,128)} %param.16) | copy-start | bytes 292
  1.7 18.9 %collective-permute-start = (bf16[512,512]{1,0:T(8,128)(2,1)S(1)}, bf16[512,512]{1,0:T(8,128)(2,1)S(1)}, u32[]{:S(2)}, u32[]{:S(2)}) collective-permute-start(bf16[512,512]{1,0:T(8,128)(2,1)S(1)} %slice.15), channel_id=1, source_target_pairs={{0,2},{1,3},{2,0},{3,1},{4,6},{5,7},{6,4},{7,5},{8,10},{9,11},{10,... | collective-permute-start | bytes 1572872 | tf_op jit(solution)/shard_map/ppermute | solution.py:274
  20.6 38.3 %all-to-all-start = ((bf16[8,96,896]{2,1,0:T(8,128)(2,1)}), bf16[8,96,896]{2,1,0:T(8,128)(2,1)S(1)}, u32[]{:S(2)}, u32[]{:S(2)}) async-start(bf16[8,96,896]{2,1,0:T(8,128)(2,1)} %bitcast.44), calls=%async_computation | async-start | bytes 2752512 | tf_op jit(solution)/shard_map/all_to_all | solution.py:277
  29.8 48.6 %collective-permute-start.3 = (bf16[512,1536]{1,0:T(8,128)(2,1)}, bf16[512,1536]{1,0:T(8,128)(2,1)S(1)}, u32[]{:S(2)}, u32[]{:S(2)}) collective-permute-start(bf16[512,1536]{1,0:T(8,128)(2,1)} %slice.17), channel_id=1, source_target_pairs={{0,2},{1,3},{2,0},{3,1},{4,6},{5,7},{6,4},{7,5},{8,10},{9,11},{10,... | collective-permute-start | bytes 4718600 | tf_op jit(solution)/shard_map/ppermute | solution.py:276
  58.9 1.1 %copy-start.2 = (bf16[8,96,896]{2,1,0:T(8,128)(2,1)}, bf16[8,96,896]{2,1,0:T(8,128)(2,1)S(1)}, u32[]{:S(2)}) copy-start(bf16[8,96,896]{2,1,0:T(8,128)(2,1)S(1)} %all-to-all-done) | copy-start | bytes 4128772
  67.3 3.8 %copy-start.1 = (bf16[512,3584]{1,0:T(8,128)(2,1)S(1)}, bf16[512,3584]{1,0:T(8,128)(2,1)}, u32[]{:S(2)}) copy-start(bf16[512,3584]{1,0:T(8,128)(2,1)} %param.25) | copy-start | bytes 11010052
  68.5 9.6 %collective-permute-start.1 = (bf16[2,192,512]{2,1,0:T(8,128)(2,1)S(1)}, bf16[2,192,512]{2,1,0:T(8,128)(2,1)S(1)}, u32[]{:S(2)}, u32[]{:S(2)}) collective-permute-start(bf16[2,192,512]{2,1,0:T(8,128)(2,1)S(1)} %dynamic-slice_bitcast_fusion), channel_id=1, source_target_pairs={{0,2},{1,3},{2,0},{3,1},{4,6},{5,7},{6,4},{7,5},{8,10},{9,11},{10,... | collective-permute-start | bytes 1179656 | tf_op jit(solution)/shard_map/ppermute | solution.py:212
  71.1 1.6 %copy-start.3 = (bf16[768,512]{1,0:T(8,128)(2,1)S(1)}, bf16[768,512]{1,0:T(8,128)(2,1)}, u32[]{:S(2)}) copy-start(bf16[768,512]{1,0:T(8,128)(2,1)} %get-tuple-element.8) | copy-start | bytes 2359300
  72.6 6.9 %collective-permute-start.6 = (bf16[192,1536]{1,0:T(8,128)(2,1)S(1)}, bf16[192,1536]{1,0:T(8,128)(2,1)S(1)}, u32[]{:S(2)}, u32[]{:S(2)}) collective-permute-start(bf16[192,1536]{1,0:T(8,128)(2,1)S(1)} %convolution_convert_fusion), channel_id=1, source_target_pairs={{0,1},{1,0},{2,3},{3,2},{4,5},{5,4},{6,7},{7,6},{8,9},{9,8},{10,11... | collective-permute-start | bytes 1769480 | tf_op jit(solution)/shard_map/ppermute | solution.py:213
  74.6 8.0 %collective-permute-start.5 = (bf16[192,1536]{1,0:T(8,128)(2,1)S(1)}, bf16[192,1536]{1,0:T(8,128)(2,1)S(1)}, u32[]{:S(2)}, u32[]{:S(2)}) collective-permute-start(bf16[192,1536]{1,0:T(8,128)(2,1)S(1)} %convolution_convert_fusion.1), channel_id=1, source_target_pairs={{0,1},{1,0},{2,3},{3,2},{4,5},{5,4},{6,7},{7,6},{8,9},{9,8},{10,11... | collective-permute-start | bytes 1769480 | tf_op jit(solution)/shard_map/ppermute | solution.py:225
  78.3 3.5 %collective-permute-start.2 = (bf16[192,512]{1,0:T(8,128)(2,1)S(1)}, bf16[192,512]{1,0:T(8,128)(2,1)S(1)}, u32[]{:S(2)}, u32[]{:S(2)}) collective-permute-start(bf16[192,512]{1,0:T(8,128)(2,1)S(1)} %fusion.9), channel_id=1, source_target_pairs={{0,1},{1,0},{2,3},{3,2},{4,5},{5,4},{6,7},{7,6},{8,9},{9,8},{10,11... | collective-permute-start | bytes 589832 | tf_op jit(solution)/shard_map/ppermute | solution.py:229
  78.9 3.2 %collective-permute-start.4 = (bf16[192,1536]{1,0:T(8,128)(2,1)S(1)}, bf16[192,1536]{1,0:T(8,128)(2,1)S(1)}, u32[]{:S(2)}, u32[]{:S(2)}) collective-permute-start(bf16[192,1536]{1,0:T(8,128)(2,1)S(1)} %fusion.2), channel_id=1, source_target_pairs={{0,1},{1,0},{2,3},{3,2},{4,5},{5,4},{6,7},{7,6},{8,9},{9,8},{10,11... | collective-permute-start | bytes 1769480 | tf_op jit(solution)/shard_map/ppermute | solution.py:229
  79.9 15.3 %collective-permute-start.7 = (bf16[192,1536]{1,0:T(8,128)(2,1)S(1)}, bf16[192,1536]{1,0:T(8,128)(2,1)S(1)}, u32[]{:S(2)}, u32[]{:S(2)}) collective-permute-start(bf16[192,1536]{1,0:T(8,128)(2,1)S(1)} %add_convert_fusion.1), channel_id=1, source_target_pairs={{0,2},{1,3},{2,0},{3,1},{4,6},{5,7},{6,4},{7,5},{8,10},{9,11},{10,... | collective-permute-start | bytes 1769480 | tf_op jit(solution)/shard_map/ppermute | solution.py:217

commit v4 on v3

--- a/solution.py
+++ b/solution.py
@@ -214,7 +214,8 @@
         product(one(away, 1 - core), tail_weight).astype(jnp.bfloat16), "seq", near
     )
     for_far = product(one(away, core), tail_weight) + from_near.astype(jnp.float32)
-    from_far = lax.ppermute(for_far.astype(jnp.bfloat16), "seq", far)
+    for_far, home = lax.optimization_barrier((for_far.astype(jnp.bfloat16), home))
+    from_far = lax.ppermute(for_far, "seq", far)
 
     def head_sum(which):
         return [

time: 97.1 us -> 135 us (1.39)
  waiting for transfers between devices: 44.1 us -> 84.8 us
  local copies, waits for them, and re-layouts: 10.6 us -> 8.43 us
    ppermute x1, waiting for transfers between devices: 0.01 us -> 31.1 us  [per_device(): far_weights = (far_first, lax.ppermute(later[:, first:early], 'seq', far))]
    ppermute x1, waiting for transfers between devices: 2.84 us -> 7.93 us  [sum_groups(): far_context = lax.ppermute(away, 'seq', far)]
    all_to_all x1, waiting for transfers between devices: 28.6 us -> 31.8 us  [per_device(): lax.all_to_all(send.reshape(peer_count, capacity, cols + META), 'dp', spl...]
  transfers between devices with their start and end apart: 9 -> 9, of which waited for: 3 -> 5; matrix products, arithmetic and copies ran while one was open for 16% -> 8% of each run, Pallas kernels for 21% -> 10%
where the time goes in v4:
time: 135 us
  waiting for transfers between devices  84.8 us (63%)
  Pallas kernels  20.6 us (15%)
  starting transfers between devices  12.3 us (9%)
  local copies, waits for them, and re-layouts  8.43 us (6%)
  matrix products  6.61 us (5%)
  other arithmetic  1.4 us (1%)
    all_to_all x1, waiting for transfers between devices, per_device(): lax.all_to_all(send.reshape(peer_count, capacity, cols + META), 'dp', spl...  31.8 us
    ppermute x1, waiting for transfers between devices, per_device(): far_weights = (far_first, lax.ppermute(later[:, first:early], 'seq', far))  31.1 us
    ppermute x1, waiting for transfers between devices, sum_groups(): from_far = lax.ppermute(for_far, 'seq', far)  13.5 us
    pallas_call x1, Pallas kernels, per_device(): pl.pallas_call(lambda *refs: send_kernel(capacity, width, *refs), name='p...  13.3 us
    ppermute x1, waiting for transfers between devices, sum_groups(): far_context = lax.ppermute(away, 'seq', far)  7.93 us
    pallas_call x1, Pallas kernels, per_device(): pl.pallas_call(lambda *refs: attend_kernel(float(peer_count * rows), kv_c...  7.29 us
    dot_general x12, matrix products, product(): return jnp.dot(rows, weight, preferred_element_type=jnp.float32)  6.61 us
    all_to_all x1, starting transfers between devices, per_device(): lax.all_to_all(send.reshape(peer_count, capacity, cols + META), 'dp', spl...  5.82 us
  transfers between devices with their start and end apart: 9, of which 5 were waited for; matrix products, arithmetic and copies ran while one was open for 8% of the time, Pallas kernels for 10%

profile of v4, /device:TPU:0, one launch (start us, length us, event | category | flops | bytes accessed | tf_op | source)
XLA Modules:
  0.0 135.0 jit_solution(4902532696161609843)
XLA Ops:
  0.6 0.0 copy-start
  0.6 1.1 slice.15
  1.7 3.1 %collective-permute-start = (bf16[512,512]{1,0:T(8,128)(2,1)S(1)}, bf16[512,512]{1,0:T(8,128)(2,1)S(1)}, u32[]{:S(2)}, u32[]{:S(2)}) collective-permute-start(bf16[512,512]{1,0:T(8,128)(2,1)S(1)} %slice.15), channel_id=1, source_target_pairs={{0,2},{1,3},{2,0},{3,1},{4,6},{5,7},{6,4},{7,5},{8,10},{9,11},{10,... | collective-permute-start | bytes 1572872 | tf_op jit(solution)/shard_map/ppermute | solution.py:275
  4.8 1.3 broadcast_in_dim.6.refs_9_
  6.1 1.3 broadcast_in_dim.7.refs_10_
  7.3 13.3 %project_and_pack.1 = bf16[768,896]{1,0:T(8,128)(2,1)} custom-call(bf16[576,3584]{1,0:T(8,128)(2,1)} %refs_0_.1, f32[28,128]{1,0:T(8,128)} %bitcast.51, bf16[3584,512]{1,0:T(8,128)(2,1)} %refs_2_.1, bf16[3584,128]{1,0:T(8,128)(2,1)} %refs_3_.1, bf16[3584,128]{1,0:T(8,128)(2,1)} %refs_4_.1, f32[4,128]{1,0:T(4,128)} %bitcast.52, f32[1,128]{1,0:T(1,128)} %bitcast.54, ...), custom_call_target="tpu_custom_call" | custom-call | tf_op jit(solution)/shard_map/project_and_pack/pallas_call | solution.py:255
  20.6 0.0 collective-permute-done
  20.6 5.8 %all-to-all-start = ((bf16[8,96,896]{2,1,0:T(8,128)(2,1)}), bf16[8,96,896]{2,1,0:T(8,128)(2,1)S(1)}, u32[]{:S(2)}, u32[]{:S(2)}) async-start(bf16[8,96,896]{2,1,0:T(8,128)(2,1)} %bitcast.46), calls=%async_computation | async-start | bytes 2752512 | tf_op jit(solution)/shard_map/all_to_all | solution.py:278
  26.4 0.0 copy-done
  26.4 0.7 fusion.56.refs_0_
  27.1 31.8 %all-to-all-done = bf16[8,96,896]{2,1,0:T(8,128)(2,1)S(1)} async-done(((bf16[8,96,896]{2,1,0:T(8,128)(2,1)}), bf16[8,96,896]{2,1,0:T(8,128)(2,1)S(1)}, u32[]{:S(2)}, u32[]{:S(2)}) %all-to-all-start) | async-done | bytes 1376288 | tf_op jit(solution)/shard_map/all_to_all | solution.py:278
  58.9 0.0 copy-start.2
  58.9 1.1 copy-done.2
  60.0 7.3 %place_and_attend.1 = (bf16[768,512]{1,0:T(8,128)(2,1)}, f32[1,768]{1,0:T(1,128)}) custom-call(s32[3]{0:T(128)} %fusion.56.refs_0_, bf16[768,896]{1,0:T(8,128)(2,1)} %bitcast.47), custom_call_target="tpu_custom_call" | custom-call | tf_op jit(solution)/shard_map/place_and_attend/pallas_call | solution.py:282
  67.3 0.0 copy-start.3
  67.3 2.1 %convolution_convert_fusion.1 = bf16[192,1536]{1,0:T(8,128)(2,1)S(1)} fusion(bf16[512,3584]{1,0:T(8,128)(2,1)} %param.25, bf16[2,2,192,512]{3,2,1,0:T(8,128)(2,1)} %bitcast.48, s32[]{:T(128)S(6)} %select_n.50, s32[]{:T(128)S(6)} %select_n.55), kind=kOutput, calls=%fused_computation.6 | convolution fusion | flops 302284800 | bytes 2359304 | tf_op jit(solution)/shard_map/dot_general | solution.py:190
  69.4 0.1 collective-permute-start.1
  69.5 0.0 copy-start.1
  69.5 1.7 %slice.18 = bf16[512,1536]{1,0:T(8,128)(2,1)S(1)} slice(bf16[512,3584]{1,0:T(8,128)(2,1)} %param.25), slice={[0:512], [512:2048]} | slice | bytes 3145728 | tf_op jit(solution)/shard_map/slice | solution.py:277
  71.1 0.6 collective-permute-start.4
  71.7 0.0 copy-done.3
  71.7 0.1 dynamic-slice_bitcast_fusion
  71.8 1.6 %collective-permute-start.2 = (bf16[2,192,512]{2,1,0:T(8,128)(2,1)S(1)}, bf16[2,192,512]{2,1,0:T(8,128)(2,1)S(1)}, u32[]{:S(2)}, u32[]{:S(2)}) collective-permute-start(bf16[2,192,512]{2,1,0:T(8,128)(2,1)S(1)} %get-tuple-element.16), channel_id=1, source_target_pairs={{0,2},{1,3},{2,0},{3,1},{4,6},{5,7},{6,4},{7,5},{8,10},{9,11},{10,... | collective-permute-start | bytes 1179656 | tf_op jit(solution)/shard_map/ppermute | solution.py:212
  73.3 1.3 constant_dynamic-slice_fusion
  74.6 0.0 collective-permute-done.1
  74.7 0.0 copy-done.1
  74.7 0.5 add_convert_fusion.1
  75.2 0.5 convolution_convert_fusion
  75.7 0.5 fusion.3
  76.2 0.5 fusion.5
  76.7 0.3 fusion.22
  76.9 0.5 fusion.11
  77.4 31.1 %collective-permute-done.4 = bf16[512,1536]{1,0:T(8,128)(2,1)S(1)} collective-permute-done((bf16[512,1536]{1,0:T(8,128)(2,1)S(1)}, bf16[512,1536]{1,0:T(8,128)(2,1)S(1)}, u32[]{:S(2)}, u32[]{:S(2)}) %collective-permute-start.4) | collective-permute-done | bytes 1572896 | tf_op jit(solution)/shard_map/ppermute | solution.py:277
  108.5 7.9 %collective-permute-done.2 = bf16[2,192,512]{2,1,0:T(8,128)(2,1)S(1)} collective-permute-done((bf16[2,192,512]{2,1,0:T(8,128)(2,1)S(1)}, bf16[2,192,512]{2,1,0:T(8,128)(2,1)S(1)}, u32[]{:S(2)}, u32[]{:S(2)}) %collective-permute-start.2) | collective-permute-done | bytes 393248 | tf_op jit(solution)/shard_map/ppermute | solution.py:212
  116.4 0.5 fusion.2
  116.9 0.1 collective-permute-start.5
  117.0 0.3 fusion.9
  117.3 0.6 collective-permute-start.3
  117.8 0.1 collective-permute-start.6
  117.9 0.5 collective-permute-start.7
  118.4 0.3 fusion.28
  118.7 0.6 collective-permute-done.3
  119.3 0.3 fusion.8
  119.5 0.0 collective-permute-done.5
  119.5 0.5 fusion.1
  120.1 0.0 collective-permute-done.6
  120.1 13.5 %collective-permute-done.7 = bf16[192,1536]{1,0:T(8,128)(2,1)S(1)} collective-permute-done((bf16[192,1536]{1,0:T(8,128)(2,1)S(1)}, bf16[192,1536]{1,0:T(8,128)(2,1)S(1)}, u32[]{:S(2)}, u32[]{:S(2)}) %collective-permute-start.7) | collective-permute-done | bytes 589856 | tf_op jit(solution)/shard_map/ppermute | solution.py:218
  133.6 0.2 add_convert_fusion
  133.8 1.2 pad_maximum_fusion
Async XLA Ops:
  0.6 25.8 %copy-start = (s32[8,3]{0,1:T(4,128)S(1)}, s32[8,3]{0,1:T(4,128)}, u32[]{:S(2)}) copy-start(s32[8,3]{0,1:T(4,128)} %param.16) | copy-start | bytes 292
  1.7 18.9 %collective-permute-start = (bf16[512,512]{1,0:T(8,128)(2,1)S(1)}, bf16[512,512]{1,0:T(8,128)(2,1)S(1)}, u32[]{:S(2)}, u32[]{:S(2)}) collective-permute-start(bf16[512,512]{1,0:T(8,128)(2,1)S(1)} %slice.15), channel_id=1, source_target_pairs={{0,2},{1,3},{2,0},{3,1},{4,6},{5,7},{6,4},{7,5},{8,10},{9,11},{10,... | collective-permute-start | bytes 1572872 | tf_op jit(solution)/shard_map/ppermute | solution.py:275
  20.6 38.3 %all-to-all-start = ((bf16[8,96,896]{2,1,0:T(8,128)(2,1)}), bf16[8,96,896]{2,1,0:T(8,128)(2,1)S(1)}, u32[]{:S(2)}, u32[]{:S(2)}) async-start(bf16[8,96,896]{2,1,0:T(8,128)(2,1)} %bitcast.46), calls=%async_computation | async-start | bytes 2752512 | tf_op jit(solution)/shard_map/all_to_all | solution.py:278
  58.9 1.1 copy-start.2
  67.3 4.4 %copy-start.3 = (bf16[768,512]{1,0:T(8,128)(2,1)S(1)}, bf16[768,512]{1,0:T(8,128)(2,1)}, u32[]{:S(2)}) copy-start(bf16[768,512]{1,0:T(8,128)(2,1)} %get-tuple-element.10) | copy-start | bytes 2359300
  69.4 5.3 %collective-permute-start.1 = (bf16[192,1536]{1,0:T(8,128)(2,1)S(1)}, bf16[192,1536]{1,0:T(8,128)(2,1)S(1)}, u32[]{:S(2)}, u32[]{:S(2)}) collective-permute-start(bf16[192,1536]{1,0:T(8,128)(2,1)S(1)} %convolution_convert_fusion.1), channel_id=1, source_target_pairs={{0,1},{1,0},{2,3},{3,2},{4,5},{5,4},{6,7},{7,6},{8,9},{9,8},{10,11... | collective-permute-start | bytes 1769480 | tf_op jit(solution)/shard_map/ppermute | solution.py:213
  69.5 5.2 %copy-start.1 = (bf16[512,3584]{1,0:T(8,128)(2,1)S(1)}, bf16[512,3584]{1,0:T(8,128)(2,1)}, u32[]{:S(2)}) copy-start(bf16[512,3584]{1,0:T(8,128)(2,1)} %param.25) | copy-start | bytes 11010052
  71.1 37.3 %collective-permute-start.4 = (bf16[512,1536]{1,0:T(8,128)(2,1)S(1)}, bf16[512,1536]{1,0:T(8,128)(2,1)S(1)}, u32[]{:S(2)}, u32[]{:S(2)}) collective-permute-start(bf16[512,1536]{1,0:T(8,128)(2,1)S(1)} %slice.18), channel_id=1, source_target_pairs={{0,2},{1,3},{2,0},{3,1},{4,6},{5,7},{6,4},{7,5},{8,10},{9,11},{10,... | collective-permute-start | bytes 4718600 | tf_op jit(solution)/shard_map/ppermute | solution.py:277
  71.8 44.6 %collective-permute-start.2 = (bf16[2,192,512]{2,1,0:T(8,128)(2,1)S(1)}, bf16[2,192,512]{2,1,0:T(8,128)(2,1)S(1)}, u32[]{:S(2)}, u32[]{:S(2)}) collective-permute-start(bf16[2,192,512]{2,1,0:T(8,128)(2,1)S(1)} %get-tuple-element.16), channel_id=1, source_target_pairs={{0,2},{1,3},{2,0},{3,1},{4,6},{5,7},{6,4},{7,5},{8,10},{9,11},{10,... | collective-permute-start | bytes 1179656 | tf_op jit(solution)/shard_map/ppermute | solution.py:212
  116.9 2.6 %collective-permute-start.5 = (bf16[192,1536]{1,0:T(8,128)(2,1)S(1)}, bf16[192,1536]{1,0:T(8,128)(2,1)S(1)}, u32[]{:S(2)}, u32[]{:S(2)}) collective-permute-start(bf16[192,1536]{1,0:T(8,128)(2,1)S(1)} %fusion.2), channel_id=1, source_target_pairs={{0,1},{1,0},{2,3},{3,2},{4,5},{5,4},{6,7},{7,6},{8,9},{9,8},{10,11... | collective-permute-start | bytes 1769480 | tf_op jit(solution)/shard_map/ppermute | solution.py:230
  117.3 2.0 %collective-permute-start.3 = (bf16[192,512]{1,0:T(8,128)(2,1)S(1)}, bf16[192,512]{1,0:T(8,128)(2,1)S(1)}, u32[]{:S(2)}, u32[]{:S(2)}) collective-permute-start(bf16[192,512]{1,0:T(8,128)(2,1)S(1)} %fusion.9), channel_id=1, source_target_pairs={{0,1},{1,0},{2,3},{3,2},{4,5},{5,4},{6,7},{7,6},{8,9},{9,8},{10,11... | collective-permute-start | bytes 589832 | tf_op jit(solution)/shard_map/ppermute | solution.py:230
  117.8 2.3 %collective-permute-start.6 = (bf16[192,1536]{1,0:T(8,128)(2,1)S(1)}, bf16[192,1536]{1,0:T(8,128)(2,1)S(1)}, u32[]{:S(2)}, u32[]{:S(2)}) collective-permute-start(bf16[192,1536]{1,0:T(8,128)(2,1)S(1)} %convolution_convert_fusion), channel_id=1, source_target_pairs={{0,1},{1,0},{2,3},{3,2},{4,5},{5,4},{6,7},{7,6},{8,9},{9,8},{10,11... | collective-permute-start | bytes 1769480 | tf_op jit(solution)/shard_map/ppermute | solution.py:226
  117.9 15.7 %collective-permute-start.7 = (bf16[192,1536]{1,0:T(8,128)(2,1)S(1)}, bf16[192,1536]{1,0:T(8,128)(2,1)S(1)}, u32[]{:S(2)}, u32[]{:S(2)}) collective-permute-start(bf16[192,1536]{1,0:T(8,128)(2,1)S(1)} %add_convert_fusion.1), channel_id=1, source_target_pairs={{0,2},{1,3},{2,0},{3,1},{4,6},{5,7},{6,4},{7,5},{8,10},{9,11},{10,... | collective-permute-start | bytes 1769480 | tf_op jit(solution)/shard_map/ppermute | solution.py:218
